TPU v7x, 32 devices: a whole 2x2x4 slice. The times are simulated.
32 devices in a mesh: gx: 2 (over core), gy: 4 (over y, x), gz: 4 (over z).
Axes of the slice: x: 2, y: 2, z: 4, core: 2. Of those that a mesh axis runs over, the one named last changes fastest.
Arguments:
- displacement_start: float32 [3, 8, 64, 512], P(None, 'gx', 'gy', 'gz'), may hold values from -4 to 4
- external_force: float32 [3, 8, 64, 512], P(None, 'gx', 'gy', 'gz'), may hold values from -6 to 6
- damage_old: float32 [8, 64, 512], P('gx', 'gy', 'gz'), may hold values from 0 to 0.9
- history_old: float32 [8, 64, 512], P('gx', 'gy', 'gz'), may hold values from 0.02 to 2
- crack_labels: int32 [8, 64, 512], P('gx', 'gy', 'gz'), may hold values 0 or 1
- fixed_flags: int32 [8, 64, 512], P('gx', 'gy', 'gz'), may hold values 0 or 1
Outputs:
- displacement: float32 [3, 8, 64, 512], P(None, 'gx', 'gy', 'gz')
- damage: float32 [8, 64, 512], P('gx', 'gy', 'gz')
- history: float32 [8, 64, 512], P('gx', 'gy', 'gz')
All inputs are finite; a program needn't handle non-finite values. No bound on the sum of `crack_labels` or of `fixed_flags` on one device may be relied on, other than what follows from the above.
Results may differ from a plain program's by a relative error of at most 0.0001.
Values sent between devices are 32-bit elements; how exact they have to be, the bound alone decides.
A program may use at most 64 MiB of HBM per device.

v0:
```python
import functools
import jax
import jax.numpy as jnp
import numpy as np
from jax import lax
from jax.experimental import pallas as pl
from jax.experimental.pallas import tpu as pltpu
from jax.sharding import PartitionSpec as P

DISP_ITERS = 4
DMG_ITERS = 2


LAME_LAMBDA = 0.5769230769230769
LAME_MU = 0.38461538461538464
BULK_MODULUS = LAME_LAMBDA + 2.0 * LAME_MU / 3.0
RESIDUAL_STIFFNESS = 0.001
TOUGHNESS = 1.0
LENGTH_SCALE = 2.0
CRACK_HISTORY = 40.0


def padded_2(cells, sides, width):
    for axis, dim in sides:
        count = lax.axis_size(axis)
        ends = count - 1
        head = lax.slice_in_dim(cells, 0, width, axis=dim)
        tail = lax.slice_in_dim(cells, cells.shape[dim] - width, cells.shape[dim], axis=dim)
        cells = jnp.concatenate(
            [
                lax.ppermute(tail, axis, [(i, (i + 1) % count) for i in range(ends)]),
                cells,
                lax.ppermute(head, axis, [((i + 1) % count, i) for i in range(ends)]),
            ],
            axis=dim,
        )
    return cells


def corner_offsets(corner):
    return (corner >> 2 & 1, corner >> 1 & 1, corner & 1)


def shape_gradients(sample):
    gradient = np.zeros((3, 8))
    for corner in range(8):
        offsets = corner_offsets(corner)
        values = [sample[k] if offsets[k] else 1.0 - sample[k] for k in range(3)]
        slopes = [1.0 if offsets[k] else -1.0 for k in range(3)]
        gradient[0, corner] = slopes[0] * values[1] * values[2]
        gradient[1, corner] = values[0] * slopes[1] * values[2]
        gradient[2, corner] = values[0] * values[1] * slopes[2]
    return gradient


def strain_matrix(gradient):
    strain = np.zeros((6, 24))
    for corner in range(8):
        column = 3 * corner
        strain[0, column] = gradient[0, corner]
        strain[1, column + 1] = gradient[1, corner]
        strain[2, column + 2] = gradient[2, corner]
        strain[3, column] = gradient[1, corner]
        strain[3, column + 1] = gradient[0, corner]
        strain[4, column + 1] = gradient[2, corner]
        strain[4, column + 2] = gradient[1, corner]
        strain[5, column] = gradient[2, corner]
        strain[5, column + 2] = gradient[0, corner]
    return strain


def element_tables():
    moduli = np.zeros((6, 6))
    moduli[:3, :3] = LAME_LAMBDA
    for k in range(3):
        moduli[k, k] += 2.0 * LAME_MU
        moduli[k + 3, k + 3] = LAME_MU
    points = [0.5 - 0.5 / np.sqrt(3.0), 0.5 + 0.5 / np.sqrt(3.0)]
    stiff_table = np.zeros((24, 24))
    laplace_table = np.zeros((8, 8))
    for sample_index in range(8):
        sample = tuple((points[k] for k in corner_offsets(sample_index)))
        gradient = shape_gradients(sample)
        strain = strain_matrix(gradient)
        stiff_table += 0.125 * strain.T @ moduli @ strain
        laplace_table += 0.125 * gradient.T @ gradient
    centre_table = strain_matrix(shape_gradients((0.5, 0.5, 0.5)))
    return (
        stiff_table.astype(np.float32),
        laplace_table.astype(np.float32),
        centre_table.astype(np.float32),
    )


def corner_views(padded, element_shape):
    corner_list = []
    for corner in range(8):
        offx, offy, offz = corner_offsets(corner)
        corner_list.append(
            padded[
                ...,
                offx : offx + element_shape[0],
                offy : offy + element_shape[1],
                offz : offz + element_shape[2],
            ]
        )
    return corner_list


def assemble_nodes(pieces):
    running = None
    for corner in range(8):
        offx, offy, offz = corner_offsets(corner)
        leading = [(0, 0)] * (pieces[corner].ndim - 3)
        placed = jnp.pad(
            pieces[corner], leading + [(offx, 1 - offx), (offy, 1 - offy), (offz, 1 - offz)]
        )
        running = placed if running is None else running + placed
    return running


def line_valid(position, devices, count):
    index = position * count + jnp.arange(count + 1, dtype=jnp.int32) - 1
    return ((index >= 0) & (index <= devices * count - 2)).astype(jnp.float32)


def strain_energy(strain):
    trace = strain[0] + strain[1] + strain[2]
    deviator = strain[:3] - trace[None] / 3.0
    shear = strain[3:]
    tensile = jnp.maximum(trace, 0.0)
    return 0.5 * BULK_MODULUS * tensile * tensile + LAME_MU * (
        jnp.sum(deviator * deviator, axis=0) + 0.5 * jnp.sum(shear * shear, axis=0)
    )


def forces_to_nodes(forces, stiffness):
    pieces = [stiffness[None] * forces[3 * target : 3 * target + 3] for target in range(8)]
    return assemble_nodes(pieces)


def element_apply(padded, stiffness, stiff_table):
    element_shape = stiffness.shape
    flat = jnp.stack(corner_views(padded, element_shape)).reshape(24, -1)
    forces = jnp.dot(stiff_table, flat, precision=lax.Precision.HIGHEST).reshape(
        (24,) + element_shape
    )
    return forces_to_nodes(forces, stiffness)


def laplace_apply(padded, element_valid, laplace_table):
    element_shape = element_valid.shape
    flat = jnp.stack(corner_views(padded, element_shape)).reshape(8, -1)
    forces = jnp.dot(laplace_table, flat, precision=lax.Precision.HIGHEST).reshape(
        (8,) + element_shape
    )
    return assemble_nodes([element_valid * forces[target] for target in range(8)])


def single_pair(pair):
    return tuple(lax.psum(pair, ("gx", "gy", "gz")))


def conjugate(solutions, residuals, inverses, counts, apply_fn):
    solutions = list(solutions)
    residuals = list(residuals)
    number = len(solutions)
    steps = max(counts)

    def pair_totals(pairs):
        return [single_pair(pairs[0])]

    precs = [inverses[0] * residuals[0]]
    applied = apply_fn(precs, list(range(number)))
    pairs = pair_totals([(jnp.sum(residuals[0] * precs[0]), jnp.sum(precs[0] * applied[0]))])
    norms = [pair[0] for pair in pairs]
    lengths = [pair[0] / pair[1] for pair in pairs]
    directions = list(precs)
    alongs = list(applied)
    for step in range(steps):
        active = [i for i in range(number) if step < counts[i]]
        for i in active:
            solutions[i] = solutions[i] + lengths[i] * directions[i]
            residuals[i] = residuals[i] - lengths[i] * alongs[i]
        later = [i for i in active if step + 1 < counts[i]]
        if later:
            i = later[0]
            precs[i] = inverses[i] * residuals[i]
            images = apply_fn([precs[i] for i in later], later)
            pairs = pair_totals(
                [
                    (jnp.sum(residuals[i] * precs[i]), jnp.sum(precs[i] * images[k]))
                    for k, i in enumerate(later)
                ]
            )
            for k, i in enumerate(later):
                norm_next, curve_sum = pairs[k]
                ratio = norm_next / norms[i]
                lengths[i] = norm_next / (curve_sum - ratio * norm_next / lengths[i])
                directions[i] = precs[i] + ratio * directions[i]
                alongs[i] = images[k] + ratio * alongs[i]
                norms[i] = norm_next
    return solutions


def body_any_mesh(displacement_start, external_force, damage_old, history_old, crack_labels, fixed_flags):
    tables = element_tables()
    stiff_table = jnp.asarray(tables[0], jnp.float32)
    laplace_table = jnp.asarray(tables[1], jnp.float32)
    centre_table = jnp.asarray(tables[2], jnp.float32)
    highest = lax.Precision.HIGHEST
    size_x, size_y, size_z = damage_old.shape
    free_mask = 1.0 - fixed_flags.astype(jnp.float32)
    start_disp = displacement_start * free_mask[None]
    element_valid = (
        line_valid(lax.axis_index("gx"), lax.axis_size("gx"), size_x)[:, None, None]
        * line_valid(lax.axis_index("gy"), lax.axis_size("gy"), size_y)[None, :, None]
        * line_valid(lax.axis_index("gz"), lax.axis_size("gz"), size_z)[None, None, :]
    )
    element_shape = element_valid.shape
    start_pad = padded_2(
        jnp.concatenate([start_disp, damage_old[None]], axis=0),
        (("gx", 1), ("gy", 2), ("gz", 3)),
        1,
    )
    corner_list = corner_views(start_pad, element_shape)
    damage_mean = sum((view[3] for view in corner_list)) / 8.0
    stiffness = ((1.0 - damage_mean) ** 2 + RESIDUAL_STIFFNESS) * element_valid
    flat = jnp.stack([view[:3] for view in corner_list]).reshape(24, -1)
    combined = jnp.dot(
        jnp.concatenate([stiff_table, centre_table], axis=0), flat, precision=highest
    )
    forces = combined[:24].reshape((24,) + element_shape)
    strain = combined[24:].reshape((6,) + element_shape)
    start_image = forces_to_nodes(forces, stiffness)[:, 1:-1, 1:-1, 1:-1]
    energy = strain_energy(strain) * element_valid
    nodal_energy = assemble_nodes([energy] * 8)[1:-1, 1:-1, 1:-1] / 8.0
    history = jnp.maximum(
        jnp.maximum(history_old, nodal_energy), CRACK_HISTORY * crack_labels.astype(jnp.float32)
    )
    stiff_diag = jnp.diagonal(stiff_table)
    diag_pieces = [
        stiffness[None] * stiff_diag[3 * target : 3 * target + 3][:, None, None, None]
        for target in range(8)
    ]
    elastic_diag = assemble_nodes(diag_pieces)[:, 1:-1, 1:-1, 1:-1]
    inverse_elastic = 1.0 / (free_mask[None] * elastic_diag + (1.0 - free_mask[None]))

    def constrained(nodal_field):
        masked = free_mask[None] * nodal_field
        padded = padded_2(masked, (("gx", 1), ("gy", 2), ("gz", 3)), 1)
        nodes = element_apply(padded, stiffness, stiff_table)[:, 1:-1, 1:-1, 1:-1]
        return free_mask[None] * nodes + (1.0 - free_mask[None]) * nodal_field

    reaction = TOUGHNESS / LENGTH_SCALE + 2.0 * history
    laplace_diag = assemble_nodes(
        [element_valid * laplace_table[target, target] for target in range(8)]
    )[1:-1, 1:-1, 1:-1]
    inverse_damage = 1.0 / (TOUGHNESS * LENGTH_SCALE * laplace_diag + reaction)
    residual = free_mask[None] * (external_force - start_image)
    start_lap = laplace_apply(start_pad[3], element_valid, laplace_table)[1:-1, 1:-1, 1:-1]
    damage_residual = 2.0 * history - (TOUGHNESS * LENGTH_SCALE * start_lap + reaction * damage_old)

    def damage_operator(nodal_field):
        padded = padded_2(nodal_field, (("gx", 0), ("gy", 1), ("gz", 2)), 1)
        lap_nodes = laplace_apply(padded, element_valid, laplace_table)[1:-1, 1:-1, 1:-1]
        return TOUGHNESS * LENGTH_SCALE * lap_nodes + reaction * nodal_field

    def single_elastic(fields, active):
        return [constrained(fields[0])]

    def single_damage(fields, active):
        return [damage_operator(fields[0])]

    displacement = conjugate(
        [start_disp], [residual], [inverse_elastic], [DISP_ITERS], single_elastic
    )[0]
    damage = conjugate(
        [damage_old], [damage_residual], [inverse_damage], [DMG_ITERS], single_damage
    )[0]
    return (displacement, damage, history)


DEPTH = 8
SPECTRUM = 3.2
MESH = pl.DeviceIdType.MESH


def walsh_tables():
    stiff, laplace, _ = element_tables()
    signs = np.array(
        [
            [np.prod([1.0 if c >> k & 1 else (-1.0 if m >> k & 1 else 1.0) for k in range(3)]) for c in range(8)]
            for m in range(8)
        ]
    )
    wide = np.kron(signs, np.eye(3))
    stiff_modes = wide @ stiff.astype(np.float64) @ wide.T / 64.0
    laplace_modes = signs @ laplace.astype(np.float64) @ signs.T / 64.0
    return stiff_modes, laplace_modes, float(stiff[0, 0]), float(laplace[0, 0])


def kernel(
    sizes,
    disp_ref,
    force_ref,
    damage_ref,
    history_ref,
    labels_ref,
    flags_ref,
    out_disp,
    out_damage,
    out_history,
    ext,
    modes,
    basis,
    resid,
    stiff,
    inverse,
    hist,
    react,
    spread,
    dinverse,
    dbasis,
    dresid,
    zsend,
    zrecv,
    zpart,
    sums,
    ysend_sem,
    yrecv_sem,
    zsend_sem,
    zrecv_sem,
    xsend_sem,
    xrecv_sem,
    asend_sem,
    arecv_sem,
):
    ngy, ngz, lx, ly, lz = sizes
    nx = 2 * lx
    rows = ly + 2 * DEPTH
    fields = 8
    npeer = ngy * ngz
    count = fields * lx
    stiff_modes, laplace_modes, stiff_diag, laplace_diag = walsh_tables()
    gx, gy, gz = lax.axis_index("gx"), lax.axis_index("gy"), lax.axis_index("gz")
    xo = gx * lx
    other = 1 - gx
    me = gy * ngz + gz
    partner = (other, gy, gz)

    GZ = nx
    barrier = pltpu.get_barrier_semaphore()
    pl.semaphore_signal(barrier, inc=1, device_id=partner, device_id_type=MESH)
    for o in range(1, npeer):
        q = lax.rem(me + o, npeer)
        pl.semaphore_signal(barrier, inc=1, device_id=(gx, q // ngz, lax.rem(q, ngz)), device_id_type=MESH)

    for p in range(lx):
        flag = flags_ref[p].astype(jnp.float32)
        free = 1.0 - flag
        for c in range(3):
            ext[c, xo + p, 0:ly] = free * disp_ref[c, p]
            ext[3 + c, xo + p, 0:ly] = force_ref[c, p]
        ext[6, xo + p, 0:ly] = damage_ref[p]
        top = jnp.maximum(history_ref[p], CRACK_HISTORY * labels_ref[p].astype(jnp.float32))
        ext[7, xo + p, 0:ly] = top * (free - flag)
    pl.semaphore_wait(barrier, npeer)

    own = pl.ds(xo, lx)

    def xcopy(src, dst, k):
        return pltpu.make_async_remote_copy(
            src_ref=src, dst_ref=dst, send_sem=xsend_sem.at[k], recv_sem=xrecv_sem.at[k],
            device_id=partner, device_id_type=MESH,
        )

    def ycopy(src_row, dst_row, k, shift):
        return pltpu.make_async_remote_copy(
            src_ref=ext.at[:, own, src_row : src_row + DEPTH, 0:lz],
            dst_ref=ext.at[:, own, dst_row : dst_row + DEPTH, 0:lz],
            send_sem=ysend_sem.at[k], recv_sem=yrecv_sem.at[k],
            device_id=(gx, gy + shift, gz), device_id_type=MESH,
        )

    def zcopy(k, shift):
        return pltpu.make_async_remote_copy(
            src_ref=zsend.at[k], dst_ref=zrecv.at[k],
            send_sem=zsend_sem.at[k], recv_sem=zrecv_sem.at[k],
            device_id=(gx, gy, gz + shift), device_id_type=MESH,
        )

    has_down, has_up = gy > 0, gy < ngy - 1
    has_left, has_right = gz > 0, gz < ngz - 1
    send_down = ycopy(0, ly, 0, -1)
    send_up = ycopy(ly - DEPTH, ly + DEPTH, 1, 1)
    x_own = xcopy(ext.at[:, own, 0:ly, 0:lz], ext.at[:, own, 0:ly, 0:lz], 0)
    pl.when(has_down)(send_down.start)
    pl.when(has_up)(send_up.start)
    x_own.start()

    @pl.when(jnp.logical_not(has_up))
    def _():
        for p in range(lx):
            for f in range(fields):
                ext[f, xo + p, ly : ly + DEPTH] = jnp.zeros((DEPTH, lz), jnp.float32)

    @pl.when(jnp.logical_not(has_down))
    def _():
        for p in range(lx):
            for f in range(fields):
                ext[f, xo + p, ly + DEPTH : rows] = jnp.zeros((DEPTH, lz), jnp.float32)

    @pl.when(jnp.logical_not(has_right))
    def _():
        zrecv[0] = jnp.zeros((count // 16, rows, 128), jnp.float32)

    @pl.when(jnp.logical_not(has_left))
    def _():
        zrecv[1] = jnp.zeros((count // 16, rows, 128), jnp.float32)

    pl.when(has_up)(send_down.wait_recv)
    pl.when(has_down)(send_up.wait_recv)

    x_ghost = xcopy(ext.at[:, own, ly:rows, 0:lz], ext.at[:, own, ly:rows, 0:lz], 1)
    x_ghost.start()
    group = lax.broadcasted_iota(jnp.int32, (rows, 128), 1) // 8
    for j in range(count // 16):
        low = jnp.zeros((rows, 128), jnp.float32)
        high = jnp.zeros((rows, 128), jnp.float32)
        for k in range(16):
            f, p = divmod(16 * j + k, lx)
            first = ext[f, xo + p, :, 0:128]
            turned = pltpu.roll(first, (8 * k + 8) % 128, 1) if k < 15 else first
            low = jnp.where(group == (k + 1) % 16, turned, low)
            high = jnp.where(group == k, turned, high)
        zsend[0, j] = low
        zsend[1, j] = high
    z_left = zcopy(0, -1)
    z_right = zcopy(1, 1)
    pl.when(has_left)(z_left.start)
    pl.when(has_right)(z_right.start)
    pl.when(has_right)(z_left.wait_recv)
    pl.when(has_left)(z_right.wait_recv)
    x_z = xcopy(zrecv, zpart, 2)
    x_z.start()

    def unpack(source, base, into, field):
        j = field * lx // 16
        low = source[0, j]
        high = source[1, j]
        for p in range(lx):
            k = field * lx + p - 16 * j
            both = jnp.where(group == k, high, low)
            turned = pltpu.roll(both, lax.rem(16 * base + (16 * p - 8 * k) % 128, 128), 1)
            into = jnp.where(group // 2 == base + p, turned, into)
        return into

    blank = jnp.zeros((rows, 128), jnp.float32)
    half = [unpack(zrecv, xo, blank, f) for f in range(fields)]
    for f in range(fields):
        ext[f, GZ] = half[f]
    x_own.wait_recv()
    x_ghost.wait_recv()
    x_z.wait_recv()
    for f in range(fields):
        ext[f, GZ] = unpack(zpart, other * lx, ext[f, GZ], f)

    row = lax.broadcasted_iota(jnp.int32, (rows, 128), 0)
    lane = lax.broadcasted_iota(jnp.int32, (rows, 128), 1)
    inside = lane % 16
    ypos = gy * ly + jnp.where(row < ly + DEPTH, row, row - rows)
    zpos = gz * lz + lane
    zghost = gz * lz + jnp.where(inside < 8, inside - 8, inside + (lz - 8))
    yvalid = (ypos >= 0) & (ypos <= ngy * ly - 2)
    valid = jnp.where(yvalid & (zpos <= ngz * lz - 2), 1.0, 0.0)
    gvalid = jnp.where(
        yvalid & (zghost >= 0) & (zghost <= ngz * lz - 2) & (lane < 16 * (nx - 1)), 1.0, 0.0
    )

    def y_up(a):
        return pltpu.roll(a, rows - 1, 0)

    def y_dn(a):
        return pltpu.roll(a, 1, 0)

    def z_up(a, ghost, p):
        return jnp.where(lane == 127, pltpu.roll(ghost, 119 - 16 * p, 1), pltpu.roll(a, 127, 1))

    def z_up_take(acc, a, p):
        return jnp.where(lane == 16 * p + 7, pltpu.roll(a, 16 * p + 7, 1), acc)

    def z_dn(a, ghost, p):
        return jnp.where(lane == 0, pltpu.roll(ghost, 121 - 16 * p, 1), pltpu.roll(a, 1, 1))

    def z_dn_take(acc, a, p):
        return jnp.where(lane == 16 * p + 8, pltpu.roll(a, 16 * p + 9, 1), acc)

    def x_up(a):
        return pltpu.roll(a, 112, 1)

    def x_dn(a):
        return pltpu.roll(a, 16, 1)

    def forward(u, near):
        zs, zd = u + near, near - u
        a, b = y_up(zs), y_up(zd)
        return zs + a, a - zs, zd + b, b - zd

    def half_back(ss, yd, zd, yz):
        s = (ss - yd) + y_dn(ss + yd)
        d = (zd - yz) + y_dn(zd + yz)
        return s - d, s + d

    def damage_sum(p):
        a = ext[6, p]
        s = a + z_up(a, ext[6, GZ], p)
        return s + y_up(s), a

    def rigidity(low, high, mask):
        rest = 1.0 - (low + high) * 0.125
        return (rest * rest + RESIDUAL_STIFFNESS) * mask

    def g_body(p, carry):
        low, ghost = carry
        high, a = damage_sum(p + 1)
        stiff[p] = rigidity(low, high, valid)
        return high, z_up_take(ghost, a, p + 1)

    sum_first, a_first = damage_sum(0)
    g_ghost = z_up_take(pltpu.roll(ext[6, GZ], 127, 1), a_first, 0)
    _, g_ghost = lax.fori_loop(0, nx - 1, g_body, (sum_first, g_ghost), unroll=True)
    g_ghost = ext[6, GZ] + g_ghost
    g_ghost = g_ghost + y_up(g_ghost)
    stiff[GZ] = rigidity(g_ghost, x_up(g_ghost), gvalid)
    stiff[nx - 1] = blank

    def gather_back(ref, emit):
        ghost = ref[GZ]

        def step(p, carry):
            low, taken = carry
            a = ref[p]
            s = a + z_dn(a, ghost, p)
            here = s + y_dn(s)
            emit(p, low + here)
            return here, z_dn_take(taken, a, p)

        _, taken = lax.fori_loop(0, nx, step, (blank, pltpu.roll(ghost, 1, 1)), unroll=True)
        s = ghost + taken
        s = s + y_dn(s)
        emit(GZ, s + x_dn(s))

    def inv_emit(p, total):
        q = stiff_diag * total
        free = ext[7, p] > 0.0
        inverse[p] = jnp.where(free, 1.0 / jnp.where(free, q, 1.0), 0.0)

    gather_back(stiff, inv_emit)

    def pass_one(load, number):
        ghosts = [load(c, GZ) for c in range(number)]

        def step(p, taken):
            new = []
            for c in range(number):
                u = load(c, p)
                out = forward(u, z_up(u, ghosts[c], p))
                for m in range(4):
                    modes[4 * c + m, p] = out[m]
                new.append(z_up_take(taken[c], u, p))
            return tuple(new)

        taken = lax.fori_loop(0, nx, step, tuple(pltpu.roll(g, 127, 1) for g in ghosts), unroll=True)
        for c in range(number):
            out = forward(ghosts[c], taken[c])
            for m in range(4):
                modes[4 * c + m, GZ] = out[m]

    def sm(mode_a, comp_a, mode_b, comp_b):
        return float(stiff_modes[3 * mode_a + comp_a, 3 * mode_b + comp_b])

    k_lame = sm(4, 0, 2, 1)
    k_two = sm(4, 0, 4, 0) - k_lame
    k_shear = sm(2, 0, 2, 0)
    k_twist = sm(3, 0, 5, 1)
    k_bend = sm(3, 1, 3, 1)
    k_cross = sm(3, 1, 5, 0)
    k_last = sm(7, 0, 7, 0)

    def element_pass(with_energy):
        def element(low, high, g, p, r):
            S = [low[m] + high[m] if m % 4 else None for m in range(12)]
            D = [high[m] - low[m] for m in range(12)]
            xX, xXY, xXZ, xXYZ = D[0:4]
            yX, yXY, yXZ, yXYZ = D[4:8]
            zX, zXY, zXZ, zXYZ = D[8:12]
            _, xY, xZ, xYZ = S[0:4]
            _, yY, yZ, yYZ = S[4:8]
            _, zY, zZ, zYZ = S[8:12]
            div = xX + yY + zZ
            sxy, sxz, syz = xY + yX, xZ + zX, yZ + zY
            if with_energy:
                trace = 0.25 * div
                tens = jnp.maximum(trace, 0.0)
                third = trace / 3.0
                ex, ey, ez = 0.25 * xX - third, 0.25 * yY - third, 0.25 * zZ - third
                dev = ex * ex + ey * ey + ez * ez
                she = (sxy * sxy + sxz * sxz + syz * syz) * 0.0625
                energy = 0.5 * BULK_MODULUS * tens * tens + LAME_MU * (dev + 0.5 * she)
                hist[p, r, :] = jnp.where(g > 0.0, energy, 0.0)
            gl, g2, gs = k_lame * g, k_two * g, k_shear * g
            gt, gb, gc, g3 = k_twist * g, k_bend * g, k_cross * g, k_last * g
            pressure = gl * div
            fxX, fyY, fzZ = pressure + g2 * xX, pressure + g2 * yY, pressure + g2 * zZ
            txy, txz, tyz = gs * sxy, gs * sxz, gs * syz
            tw = xYZ + yXZ + zXY
            fxYZ, fyXZ, fzXY = gt * (xYZ + tw), gt * (yXZ + tw), gt * (zXY + tw)
            fyYZ, fxXZ = gb * yYZ + gc * xXZ, gb * xXZ + gc * yYZ
            fzYZ, fxXY = gb * zYZ + gc * xXY, gb * xXY + gc * zYZ
            fyXY, fzXZ = gb * yXY + gc * zXZ, gb * zXZ + gc * yXY
            FD = [
                fxX, fxXY, fxXZ, g3 * xXYZ,
                txy, fyXY, fyXZ, g3 * yXYZ,
                txz, fzXY, fzXZ, g3 * zXYZ,
            ]
            FS = [
                None, txy, txz, fxYZ,
                None, fyY, tyz, fyYZ,
                None, tyz, fzZ, fzYZ,
            ]
            lows = [(-FD[m]) if FS[m] is None else FS[m] - FD[m] for m in range(12)]
            highs = [FD[m] if FS[m] is None else FS[m] + FD[m] for m in range(12)]
            return lows, highs

        def step(chunk, carry):
            r = pl.ds(pl.multiple_of(chunk * 8, 8), 8)
            low = [modes[m, 0, r, :] for m in range(12)]
            held = None
            for p in range(nx - 1):
                high = [modes[m, p + 1, r, :] for m in range(12)]
                lows, highs = element(low, high, stiff[p, r, :], p, r)
                for m in range(12):
                    modes[m, p, r, :] = lows[m] + held[m] if p else lows[m]
                held, low = highs, high
            for m in range(12):
                modes[m, nx - 1, r, :] = held[m]
            low = [modes[m, GZ, r, :] for m in range(12)]
            lows, highs = element(low, [x_up(a) for a in low], stiff[GZ, r, :], GZ, r)
            for m in range(12):
                modes[m, GZ, r, :] = lows[m] + x_dn(highs[m])
            return carry

        lax.fori_loop(0, rows // 8, step, 0, unroll=True)

    def each_node(number, emit, carry):
        ghosts = [half_back(*(modes[4 * c + m, GZ] for m in range(4))) for c in range(number)]

        def step(p, state):
            taken, carry = state
            new, values = [], []
            for c in range(number):
                near, far = half_back(*(modes[4 * c + m, p] for m in range(4)))
                values.append(near + z_dn(far, ghosts[c][1], p))
                new.append(z_dn_take(taken[c], far, p))
            return tuple(new), emit(p, values, carry, True)

        first = tuple(pltpu.roll(g[1], 1, 1) for g in ghosts)
        taken, carry = lax.fori_loop(0, nx, step, (first, carry), unroll=True)
        emit(GZ, [ghosts[c][0] + taken[c] for c in range(number)], carry, False)
        return carry

    def fold(a):
        part = a[0:8, 0:128]
        for i in range(0, ly, 8):
            for k in range(0, lz, 128):
                if i or k:
                    part = part + a[i : i + 8, k : k + 128]
        return part

    zero = jnp.zeros((8, 128), jnp.float32)
    inner = (slice(0, ly), slice(0, lz))

    pass_one(lambda c, p: ext[c, p], 3)
    element_pass(True)

    def start_emit(p, values, dot, main):
        inv = inverse[p]
        for c in range(3):
            r = ext[3 + c, p] - values[c]
            v = inv * r
            basis[c, p] = v
            if main:
                resid[c, p] = r[inner]
                dot = dot + fold((v * r)[inner])
        return dot

    vector = [each_node(3, start_emit, zero)]
    hist[nx - 1] = blank

    def hist_emit(p, total):
        react[p] = jnp.maximum(jnp.abs(ext[7, p]), 0.125 * total)

    gather_back(hist, hist_emit)

    gram = []
    for k in range(DISP_ITERS):
        pass_one(lambda c, p, k=k: basis[3 * k + c, p], 3)
        element_pass(False)
        more = k + 1 < DISP_ITERS

        def apply_emit(p, values, carry, main, k=k, more=more):
            carry = list(carry)
            if not main and not more:
                return tuple(carry)
            inv = inverse[p] * (2.0 / SPECTRUM) if more else None
            for c in range(3):
                w = values[c]
                if main:
                    wi = w[inner]
                    for j in range(k + 1):
                        carry[j] = carry[j] + fold(basis[3 * j + c, p, 0:ly] * wi)
                if more:
                    v = inv * w - basis[3 * k + c, p]
                    if k:
                        v = 2.0 * v - basis[3 * (k - 1) + c, p]
                    basis[3 * (k + 1) + c, p] = v
                    if main:
                        carry[k + 1] = carry[k + 1] + fold(v[inner] * resid[c, p])
            return tuple(carry)

        got = each_node(3, apply_emit, (zero,) * (k + 1 + (1 if more else 0)))
        gram.append(list(got[: k + 1]))
        if more:
            vector.append(got[k + 1])

    l_one = float(laplace_modes[1, 1]) * TOUGHNESS * LENGTH_SCALE
    l_two = float(laplace_modes[3, 3]) * TOUGHNESS * LENGTH_SCALE
    l_three = float(laplace_modes[7, 7]) * TOUGHNESS * LENGTH_SCALE

    def laplace_pass(load):
        pass_one(lambda c, p: load(p), 1)

        def element(low, high, mask):
            m1, m2, m3 = l_one * mask, l_two * mask, l_three * mask
            D = [high[m] - low[m] for m in range(4)]
            F = [m1 * D[0], m2 * D[1], m2 * D[2], m3 * D[3]]
            T = [m1 * (low[1] + high[1]), m1 * (low[2] + high[2]), m2 * (low[3] + high[3])]
            lows = [-F[0]] + [T[m] - F[m + 1] for m in range(3)]
            highs = [F[0]] + [T[m] + F[m + 1] for m in range(3)]
            return lows, highs

        for chunk in range(rows // 8):
            r = slice(8 * chunk, 8 * chunk + 8)
            low = [modes[m, 0, r, :] for m in range(4)]
            held = None
            for p in range(nx - 1):
                high = [modes[m, p + 1, r, :] for m in range(4)]
                lows, highs = element(low, high, valid[r])
                for m in range(4):
                    modes[m, p, r, :] = lows[m] + held[m] if p else lows[m]
                held, low = highs, high
            for m in range(4):
                modes[m, nx - 1, r, :] = held[m]
            low = [modes[m, GZ, r, :] for m in range(4)]
            lows, highs = element(low, [x_up(a) for a in low], gvalid[r])
            for m in range(4):
                modes[m, GZ, r, :] = lows[m] + x_dn(highs[m])

    spread[...] = jnp.zeros(spread.shape, jnp.float32)
    for p in range(nx - 1):
        spread[p] = valid
    spread[GZ] = gvalid

    def spread_emit(p, total):
        reaction = TOUGHNESS / LENGTH_SCALE + 2.0 * react[p]
        dinverse[p] = 1.0 / (total * (laplace_diag * TOUGHNESS * LENGTH_SCALE) + reaction)

    gather_back(spread, spread_emit)
    laplace_pass(lambda p: ext[6, p])

    def reaction_of(p):
        return TOUGHNESS / LENGTH_SCALE + 2.0 * react[p]

    def dstart(p, values, dot, main):
        r = 2.0 * react[p] - (values[0] + reaction_of(p) * ext[6, p])
        v = dinverse[p] * r
        dbasis[0, p] = v
        if main:
            dresid[p] = r[inner]
            dot = dot + fold((v * r)[inner])
        return dot

    dvector = [each_node(1, dstart, zero)]
    dgram = []
    for k in range(DMG_ITERS):
        laplace_pass(lambda p, k=k: dbasis[k, p])
        more = k + 1 < DMG_ITERS

        def dstep(p, values, carry, main, k=k, more=more):
            carry = list(carry)
            here = dbasis[k, p]
            w = values[0] + reaction_of(p) * here
            if main:
                for j in range(k + 1):
                    carry[j] = carry[j] + fold((dbasis[j, p] * w)[inner])
            if more:
                v = dinverse[p] * w - here
                if k:
                    v = 2.0 * v - dbasis[k - 1, p]
                dbasis[k + 1, p] = v
                if main:
                    carry[k + 1] = carry[k + 1] + fold(v[inner] * dresid[p])
            return tuple(carry)

        got = each_node(1, dstep, (zero,) * (k + 1 + (1 if more else 0)))
        dgram.append(list(got[: k + 1]))
        if more:
            dvector.append(got[k + 1])

    parts = vector + dvector + [x for g in gram for x in g] + [x for g in dgram for x in g]
    at = lax.broadcasted_iota(jnp.int32, (8, 128), 1)
    packed = zero
    for i, part in enumerate(parts):
        packed = jnp.where(at == i, jnp.sum(jnp.sum(part, axis=0, keepdims=True), axis=1, keepdims=True), packed)
    sums[me] = packed

    def peer_copy(o, slot):
        q = lax.rem(me + o, npeer)
        return pltpu.make_async_remote_copy(
            src_ref=sums.at[me], dst_ref=sums.at[slot],
            send_sem=asend_sem.at[o - 1], recv_sem=arecv_sem.at[o - 1],
            device_id=(gx, q // ngz, lax.rem(q, ngz)), device_id_type=MESH,
        )

    sends = [peer_copy(o, me) for o in range(1, npeer)]
    for s in sends:
        s.start()
    for p in range(lx):
        out_history[p] = react[xo + p, 0:ly]
    for o in range(1, npeer):
        peer_copy(o, lax.rem(me + npeer - o, npeer)).wait_recv()
    whole = sums[0]
    for i in range(1, npeer):
        whole = whole + sums[i]

    values = [
        jnp.sum(jnp.where(at[0:1] == i, whole[0:1], 0.0), axis=1, keepdims=True)
        for i in range(len(parts))
    ]
    nd, ng = DISP_ITERS, DMG_ITERS

    def solve(rhs, lower):
        n = len(rhs)
        A = [[lower[max(i, j)][min(i, j)] for j in range(n)] for i in range(n)]
        b = list(rhs)
        for i in range(n):
            pivot = 1.0 / A[i][i]
            for r in range(i + 1, n):
                ratio = A[r][i] * pivot
                for c in range(i + 1, n):
                    A[r][c] = A[r][c] - ratio * A[i][c]
                b[r] = b[r] - ratio * b[i]
        out = [None] * n
        for i in reversed(range(n)):
            s = b[i]
            for j in range(i + 1, n):
                s = s - A[i][j] * out[j]
            out[i] = s / A[i][i]
        return out

    def triangle(flat, n):
        return [[flat[k * (k + 1) // 2 + j] for j in range(k + 1)] for k in range(n)]

    rest = values[nd + ng :]
    cut = nd * (nd + 1) // 2
    weights = solve(values[:nd], triangle(rest[:cut], nd))
    dweights = solve(values[nd : nd + ng], triangle(rest[cut:], ng))
    for p in range(lx):
        for c in range(3):
            x = ext[c, xo + p, 0:ly, 0:lz]
            for k in range(nd):
                x = x + weights[k] * basis[3 * k + c, xo + p, 0:ly, 0:lz]
            out_disp[c, p] = x
        d = ext[6, xo + p, 0:ly, 0:lz]
        for k in range(ng):
            d = d + dweights[k] * dbasis[k, xo + p, 0:ly, 0:lz]
        out_damage[p] = d

    pl.when(has_down)(send_down.wait_send)
    pl.when(has_up)(send_up.wait_send)
    pl.when(has_left)(z_left.wait_send)
    pl.when(has_right)(z_right.wait_send)
    x_own.wait_send()
    x_ghost.wait_send()
    x_z.wait_send()
    for s in sends:
        s.wait_send()


def hand_on(*refs):
    for source, target in zip(refs[:3], refs[3:]):
        target[...] = source[...]


def body_fused(sizes, *arrays):
    ngy, ngz, lx, ly, lz = sizes
    nx, rows, fields = 2 * lx, ly + 2 * DEPTH, 8
    packs = fields * lx // 16
    npeer = ngy * ngz
    f32 = jnp.float32
    wide = (nx + 1, rows, lz)
    vmem = pl.BlockSpec(memory_space=pltpu.VMEM)
    dma = pltpu.SemaphoreType.DMA
    results = pl.pallas_call(
        functools.partial(kernel, sizes),
        out_shape=(
            jax.ShapeDtypeStruct((3, lx, ly, lz), f32),
            jax.ShapeDtypeStruct((lx, ly, lz), f32),
            jax.ShapeDtypeStruct((lx, ly, lz), f32),
        ),
        in_specs=[vmem] * 6,
        out_specs=(vmem,) * 3,
        scratch_shapes=[
            pltpu.VMEM((fields,) + wide, f32),
            pltpu.VMEM((12,) + wide, f32),
            pltpu.VMEM((3 * DISP_ITERS,) + wide, f32),
            pltpu.VMEM((3, nx, ly, lz), f32),
            pltpu.VMEM(wide, f32),
            pltpu.VMEM(wide, f32),
            pltpu.VMEM(wide, f32),
            pltpu.VMEM(wide, f32),
            pltpu.VMEM(wide, f32),
            pltpu.VMEM(wide, f32),
            pltpu.VMEM((DMG_ITERS,) + wide, f32),
            pltpu.VMEM((nx, ly, lz), f32),
            pltpu.VMEM((2, packs, rows, 128), f32),
            pltpu.VMEM((2, packs, rows, 128), f32),
            pltpu.VMEM((2, packs, rows, 128), f32),
            pltpu.VMEM((npeer, 8, 128), f32),
            dma((2,)),
            dma((2,)),
            dma((2,)),
            dma((2,)),
            dma((3,)),
            dma((3,)),
            dma((npeer - 1,)),
            dma((npeer - 1,)),
        ],
        compiler_params=pltpu.CompilerParams(
            collective_id=0, has_side_effects=True, vmem_limit_bytes=60 * 1024 * 1024
        ),
    )(*arrays)
    return pl.pallas_call(
        hand_on,
        out_shape=tuple(jax.ShapeDtypeStruct(r.shape, f32) for r in results),
        in_specs=[vmem] * 3,
        out_specs=(vmem,) * 3,
    )(*results)


def solution(mesh):
    shape = dict(mesh.shape)

    def body(*arrays):
        lx, ly, lz = arrays[2].shape
        fits = shape["gx"] == 2 and shape["gy"] * shape["gz"] > 1
        fits = fits and lx == 4 and ly % 8 == 0 and lz == 128
        if fits:
            return body_fused((shape["gy"], shape["gz"], lx, ly, lz), *arrays)
        return body_any_mesh(*arrays)

    return jax.shard_map(
        body,
        mesh=mesh,
        in_specs=(
            P(None, "gx", "gy", "gz"),
            P(None, "gx", "gy", "gz"),
            P("gx", "gy", "gz"),
            P("gx", "gy", "gz"),
            P("gx", "gy", "gz"),
            P("gx", "gy", "gz"),
        ),
        out_specs=(P(None, "gx", "gy", "gz"), P("gx", "gy", "gz"), P("gx", "gy", "gz")),
        check_vma=False,
    )
```

profile of v0, /device:TPU:0, one launch (start us, length us, event | category | flops | bytes accessed | tf_op | source)
XLA Modules:
  0.0 34.7 jit_solution(6072181140952221561)
XLA Ops:
  0.6 32.5 %shard_map.85 = (f32[3,4,16,128]{3,2,1,0:T(8,128)}, f32[4,16,128]{2,1,0:T(8,128)}, f32[4,16,128]{2,1,0:T(8,128)}) custom-call(f32[3,4,16,128]{3,2,1,0:T(8,128)} %disp_ref.1, f32[3,4,16,128]{3,2,1,0:T(8,128)} %force_ref.1, f32[4,16,128]{2,1,0:T(8,128)} %damage_ref.1, f32[4,16,128]{2,1,0:T(8,128)} %history_ref.1, s32[4,16,128]{2,1,0:T(8,128)} %labels_ref.1, ...), custom_call_target="tpu_custom_call" | custom-call | tf_op jit(solution)/shard_map/pallas_call | solution.py:915
  33.2 1.6 %shard_map.86 = (f32[3,4,16,128]{3,2,1,0:T(8,128)}, f32[4,16,128]{2,1,0:T(8,128)}, f32[4,16,128]{2,1,0:T(8,128)}) custom-call(f32[3,4,16,128]{3,2,1,0:T(8,128)} %get-tuple-element.6.refs_0_, f32[4,16,128]{2,1,0:T(8,128)} %get-tuple-element.7.refs_1_, f32[4,16,128]{2,1,0:T(8,128)} %get-tuple-element.8.refs_2_), custom_call_target="tpu_custom_call" | custom-call | tf_op jit(solution)/shard_map/pallas_call | solution.py:954
where the time goes:
time: 34.9 us; the launch traced here: 34.7 us
  Pallas kernels  34.1 us (98%)
  between operations  0.64 us (2%)
    pallas_call x1, Pallas kernels, body_fused(): pl.pallas_call(functools.partial(kernel, sizes), out_shape=(jax.ShapeDtyp...  32.5 us
    pallas_call x1, Pallas kernels, body_fused(): pl.pallas_call(hand_on, out_shape=tuple((jax.ShapeDtypeStruct(r.shape, f3...  1.58 us

commit v1 on v0

v1 whole, which is shorter than its diff:
```python
import functools
import jax
import jax.numpy as jnp
import numpy as np
from jax import lax
from jax.experimental import pallas as pl
from jax.experimental.pallas import tpu as pltpu
from jax.sharding import PartitionSpec as P

DISP_ITERS = 4
DMG_ITERS = 2


LAME_LAMBDA = 0.5769230769230769
LAME_MU = 0.38461538461538464
BULK_MODULUS = LAME_LAMBDA + 2.0 * LAME_MU / 3.0
RESIDUAL_STIFFNESS = 0.001
TOUGHNESS = 1.0
LENGTH_SCALE = 2.0
CRACK_HISTORY = 40.0


def padded_2(cells, sides, width):
    for axis, dim in sides:
        count = lax.axis_size(axis)
        ends = count - 1
        head = lax.slice_in_dim(cells, 0, width, axis=dim)
        tail = lax.slice_in_dim(cells, cells.shape[dim] - width, cells.shape[dim], axis=dim)
        cells = jnp.concatenate(
            [
                lax.ppermute(tail, axis, [(i, (i + 1) % count) for i in range(ends)]),
                cells,
                lax.ppermute(head, axis, [((i + 1) % count, i) for i in range(ends)]),
            ],
            axis=dim,
        )
    return cells


def corner_offsets(corner):
    return (corner >> 2 & 1, corner >> 1 & 1, corner & 1)


def shape_gradients(sample):
    gradient = np.zeros((3, 8))
    for corner in range(8):
        offsets = corner_offsets(corner)
        values = [sample[k] if offsets[k] else 1.0 - sample[k] for k in range(3)]
        slopes = [1.0 if offsets[k] else -1.0 for k in range(3)]
        gradient[0, corner] = slopes[0] * values[1] * values[2]
        gradient[1, corner] = values[0] * slopes[1] * values[2]
        gradient[2, corner] = values[0] * values[1] * slopes[2]
    return gradient


def strain_matrix(gradient):
    strain = np.zeros((6, 24))
    for corner in range(8):
        column = 3 * corner
        strain[0, column] = gradient[0, corner]
        strain[1, column + 1] = gradient[1, corner]
        strain[2, column + 2] = gradient[2, corner]
        strain[3, column] = gradient[1, corner]
        strain[3, column + 1] = gradient[0, corner]
        strain[4, column + 1] = gradient[2, corner]
        strain[4, column + 2] = gradient[1, corner]
        strain[5, column] = gradient[2, corner]
        strain[5, column + 2] = gradient[0, corner]
    return strain


def element_tables():
    moduli = np.zeros((6, 6))
    moduli[:3, :3] = LAME_LAMBDA
    for k in range(3):
        moduli[k, k] += 2.0 * LAME_MU
        moduli[k + 3, k + 3] = LAME_MU
    points = [0.5 - 0.5 / np.sqrt(3.0), 0.5 + 0.5 / np.sqrt(3.0)]
    stiff_table = np.zeros((24, 24))
    laplace_table = np.zeros((8, 8))
    for sample_index in range(8):
        sample = tuple((points[k] for k in corner_offsets(sample_index)))
        gradient = shape_gradients(sample)
        strain = strain_matrix(gradient)
        stiff_table += 0.125 * strain.T @ moduli @ strain
        laplace_table += 0.125 * gradient.T @ gradient
    centre_table = strain_matrix(shape_gradients((0.5, 0.5, 0.5)))
    return (
        stiff_table.astype(np.float32),
        laplace_table.astype(np.float32),
        centre_table.astype(np.float32),
    )


def corner_views(padded, element_shape):
    corner_list = []
    for corner in range(8):
        offx, offy, offz = corner_offsets(corner)
        corner_list.append(
            padded[
                ...,
                offx : offx + element_shape[0],
                offy : offy + element_shape[1],
                offz : offz + element_shape[2],
            ]
        )
    return corner_list


def assemble_nodes(pieces):
    running = None
    for corner in range(8):
        offx, offy, offz = corner_offsets(corner)
        leading = [(0, 0)] * (pieces[corner].ndim - 3)
        placed = jnp.pad(
            pieces[corner], leading + [(offx, 1 - offx), (offy, 1 - offy), (offz, 1 - offz)]
        )
        running = placed if running is None else running + placed
    return running


def line_valid(position, devices, count):
    index = position * count + jnp.arange(count + 1, dtype=jnp.int32) - 1
    return ((index >= 0) & (index <= devices * count - 2)).astype(jnp.float32)


def strain_energy(strain):
    trace = strain[0] + strain[1] + strain[2]
    deviator = strain[:3] - trace[None] / 3.0
    shear = strain[3:]
    tensile = jnp.maximum(trace, 0.0)
    return 0.5 * BULK_MODULUS * tensile * tensile + LAME_MU * (
        jnp.sum(deviator * deviator, axis=0) + 0.5 * jnp.sum(shear * shear, axis=0)
    )


def forces_to_nodes(forces, stiffness):
    pieces = [stiffness[None] * forces[3 * target : 3 * target + 3] for target in range(8)]
    return assemble_nodes(pieces)


def element_apply(padded, stiffness, stiff_table):
    element_shape = stiffness.shape
    flat = jnp.stack(corner_views(padded, element_shape)).reshape(24, -1)
    forces = jnp.dot(stiff_table, flat, precision=lax.Precision.HIGHEST).reshape(
        (24,) + element_shape
    )
    return forces_to_nodes(forces, stiffness)


def laplace_apply(padded, element_valid, laplace_table):
    element_shape = element_valid.shape
    flat = jnp.stack(corner_views(padded, element_shape)).reshape(8, -1)
    forces = jnp.dot(laplace_table, flat, precision=lax.Precision.HIGHEST).reshape(
        (8,) + element_shape
    )
    return assemble_nodes([element_valid * forces[target] for target in range(8)])


def single_pair(pair):
    return tuple(lax.psum(pair, ("gx", "gy", "gz")))


def conjugate(solutions, residuals, inverses, counts, apply_fn):
    solutions = list(solutions)
    residuals = list(residuals)
    number = len(solutions)
    steps = max(counts)

    def pair_totals(pairs):
        return [single_pair(pairs[0])]

    precs = [inverses[0] * residuals[0]]
    applied = apply_fn(precs, list(range(number)))
    pairs = pair_totals([(jnp.sum(residuals[0] * precs[0]), jnp.sum(precs[0] * applied[0]))])
    norms = [pair[0] for pair in pairs]
    lengths = [pair[0] / pair[1] for pair in pairs]
    directions = list(precs)
    alongs = list(applied)
    for step in range(steps):
        active = [i for i in range(number) if step < counts[i]]
        for i in active:
            solutions[i] = solutions[i] + lengths[i] * directions[i]
            residuals[i] = residuals[i] - lengths[i] * alongs[i]
        later = [i for i in active if step + 1 < counts[i]]
        if later:
            i = later[0]
            precs[i] = inverses[i] * residuals[i]
            images = apply_fn([precs[i] for i in later], later)
            pairs = pair_totals(
                [
                    (jnp.sum(residuals[i] * precs[i]), jnp.sum(precs[i] * images[k]))
                    for k, i in enumerate(later)
                ]
            )
            for k, i in enumerate(later):
                norm_next, curve_sum = pairs[k]
                ratio = norm_next / norms[i]
                lengths[i] = norm_next / (curve_sum - ratio * norm_next / lengths[i])
                directions[i] = precs[i] + ratio * directions[i]
                alongs[i] = images[k] + ratio * alongs[i]
                norms[i] = norm_next
    return solutions


def body_any_mesh(displacement_start, external_force, damage_old, history_old, crack_labels, fixed_flags):
    tables = element_tables()
    stiff_table = jnp.asarray(tables[0], jnp.float32)
    laplace_table = jnp.asarray(tables[1], jnp.float32)
    centre_table = jnp.asarray(tables[2], jnp.float32)
    highest = lax.Precision.HIGHEST
    size_x, size_y, size_z = damage_old.shape
    free_mask = 1.0 - fixed_flags.astype(jnp.float32)
    start_disp = displacement_start * free_mask[None]
    element_valid = (
        line_valid(lax.axis_index("gx"), lax.axis_size("gx"), size_x)[:, None, None]
        * line_valid(lax.axis_index("gy"), lax.axis_size("gy"), size_y)[None, :, None]
        * line_valid(lax.axis_index("gz"), lax.axis_size("gz"), size_z)[None, None, :]
    )
    element_shape = element_valid.shape
    start_pad = padded_2(
        jnp.concatenate([start_disp, damage_old[None]], axis=0),
        (("gx", 1), ("gy", 2), ("gz", 3)),
        1,
    )
    corner_list = corner_views(start_pad, element_shape)
    damage_mean = sum((view[3] for view in corner_list)) / 8.0
    stiffness = ((1.0 - damage_mean) ** 2 + RESIDUAL_STIFFNESS) * element_valid
    flat = jnp.stack([view[:3] for view in corner_list]).reshape(24, -1)
    combined = jnp.dot(
        jnp.concatenate([stiff_table, centre_table], axis=0), flat, precision=highest
    )
    forces = combined[:24].reshape((24,) + element_shape)
    strain = combined[24:].reshape((6,) + element_shape)
    start_image = forces_to_nodes(forces, stiffness)[:, 1:-1, 1:-1, 1:-1]
    energy = strain_energy(strain) * element_valid
    nodal_energy = assemble_nodes([energy] * 8)[1:-1, 1:-1, 1:-1] / 8.0
    history = jnp.maximum(
        jnp.maximum(history_old, nodal_energy), CRACK_HISTORY * crack_labels.astype(jnp.float32)
    )
    stiff_diag = jnp.diagonal(stiff_table)
    diag_pieces = [
        stiffness[None] * stiff_diag[3 * target : 3 * target + 3][:, None, None, None]
        for target in range(8)
    ]
    elastic_diag = assemble_nodes(diag_pieces)[:, 1:-1, 1:-1, 1:-1]
    inverse_elastic = 1.0 / (free_mask[None] * elastic_diag + (1.0 - free_mask[None]))

    def constrained(nodal_field):
        masked = free_mask[None] * nodal_field
        padded = padded_2(masked, (("gx", 1), ("gy", 2), ("gz", 3)), 1)
        nodes = element_apply(padded, stiffness, stiff_table)[:, 1:-1, 1:-1, 1:-1]
        return free_mask[None] * nodes + (1.0 - free_mask[None]) * nodal_field

    reaction = TOUGHNESS / LENGTH_SCALE + 2.0 * history
    laplace_diag = assemble_nodes(
        [element_valid * laplace_table[target, target] for target in range(8)]
    )[1:-1, 1:-1, 1:-1]
    inverse_damage = 1.0 / (TOUGHNESS * LENGTH_SCALE * laplace_diag + reaction)
    residual = free_mask[None] * (external_force - start_image)
    start_lap = laplace_apply(start_pad[3], element_valid, laplace_table)[1:-1, 1:-1, 1:-1]
    damage_residual = 2.0 * history - (TOUGHNESS * LENGTH_SCALE * start_lap + reaction * damage_old)

    def damage_operator(nodal_field):
        padded = padded_2(nodal_field, (("gx", 0), ("gy", 1), ("gz", 2)), 1)
        lap_nodes = laplace_apply(padded, element_valid, laplace_table)[1:-1, 1:-1, 1:-1]
        return TOUGHNESS * LENGTH_SCALE * lap_nodes + reaction * nodal_field

    def single_elastic(fields, active):
        return [constrained(fields[0])]

    def single_damage(fields, active):
        return [damage_operator(fields[0])]

    displacement = conjugate(
        [start_disp], [residual], [inverse_elastic], [DISP_ITERS], single_elastic
    )[0]
    damage = conjugate(
        [damage_old], [damage_residual], [inverse_damage], [DMG_ITERS], single_damage
    )[0]
    return (displacement, damage, history)


SPECTRUM = 3.2
TILE = 8
GHOST = 4
DEEP = (0, 1, 2, 6)
TURNED = (0, 3)
MESH = pl.DeviceIdType.MESH


def walsh_tables():
    stiff, laplace, _ = element_tables()
    signs = np.array(
        [
            [np.prod([1.0 if c >> k & 1 else (-1.0 if m >> k & 1 else 1.0) for k in range(3)]) for c in range(8)]
            for m in range(8)
        ]
    )
    wide = np.kron(signs, np.eye(3))
    stiff_modes = wide @ stiff.astype(np.float64) @ wide.T / 64.0
    return stiff_modes, float(stiff[0, 0]), float(laplace[0, 0])


def kernel(
    sizes,
    disp_in,
    force_in,
    damage_in,
    history_in,
    labels_in,
    flags_in,
    out_disp,
    out_damage,
    out_history,
    disp_ref,
    force_ref,
    damage_ref,
    history_ref,
    labels_ref,
    flags_ref,
    own,
    part,
    down_send,
    up_send,
    from_up,
    from_down,
    part_up,
    part_down,
    zsend,
    zrecv,
    zpart,
    gz_wide,
    gz_rows,
    modes,
    basis,
    images,
    resid,
    stiff,
    inverse,
    hist,
    react,
    dinverse,
    dbasis,
    dresid,
    sums,
    in_sem,
    ysend_sem,
    yrecv_sem,
    zsend_sem,
    zrecv_sem,
    csend_sem,
    crecv_sem,
    xsend_sem,
    xrecv_sem,
    asend_sem,
    arecv_sem,
    hop_sem,
):
    ngy, ngz, lx, ly, lz = sizes
    nx = 2 * lx
    fields = 8
    npeer = ngy * ngz
    pairs = fields * lx // 2
    packs = fields * lx // 16
    extras = len(DEEP) * lx // TILE
    wide, rows = ly + 2 * TILE, ly + TILE
    GZ = nx
    f32 = jnp.float32
    stiff_modes, stiff_diag, laplace_diag = walsh_tables()
    gx, gy, gz = lax.axis_index("gx"), lax.axis_index("gy"), lax.axis_index("gz")
    me = gy * ngz + gz
    partner = (1 - gx, gy, gz)

    def there(dy, dz):
        y, z = gy + dy, gz + dz
        return (y >= 0) & (y < ngy) & (z >= 0) & (z < ngz)

    near = [(dy, dz) for dy in (-1, 0, 1) for dz in (-1, 0, 1) if dy or dz]
    number_near = sum(there(dy, dz).astype(jnp.int32) for dy, dz in near)

    barrier = pltpu.get_barrier_semaphore()

    def greet(semaphore):
        for dy, dz in near:

            @pl.when(there(dy, dz))
            def _():
                pl.semaphore_signal(
                    semaphore, inc=1, device_id=(gx, gy + dy, gz + dz), device_id_type=MESH
                )

    greet(barrier)
    pl.semaphore_signal(barrier, inc=1, device_id=partner, device_id_type=MESH)

    loads = [
        pltpu.make_async_copy(source, target, in_sem.at[i])
        for i, (source, target) in enumerate(
            [
                (flags_in, flags_ref),
                (disp_in, disp_ref),
                (force_in, force_ref),
                (damage_in, damage_ref),
                (history_in, history_ref),
                (labels_in, labels_ref),
            ]
        )
    ]
    for load in loads:
        load.start()

    for dz, side in ((1, 0), (-1, 1)):
        for dy, low, high in ((0, 0, ly), (1, ly, ly + TILE), (-1, ly + TILE, wide)):

            @pl.when(jnp.logical_not(there(dy, dz)))
            def _():
                zrecv[side, :, low:high] = jnp.zeros((packs, high - low, 128), f32)

    @pl.when(jnp.logical_not(there(1, 0)))
    def _():
        from_up[...] = jnp.zeros(from_up.shape, f32)

    @pl.when(jnp.logical_not(there(-1, 0)))
    def _():
        from_down[...] = jnp.zeros(from_down.shape, f32)

    for load in loads:
        load.wait()

    sign = (1 - 2 * gx).astype(f32)

    def place(q):
        return q + gx * (lx - 1 - 2 * q)

    values = []
    for q in range(lx):
        p = place(q)
        flag = flags_ref[p].astype(f32)
        free = 1.0 - flag
        top = jnp.maximum(history_ref[p], CRACK_HISTORY * labels_ref[p].astype(f32))
        here = [
            free * disp_ref[0, p] * sign,
            free * disp_ref[1, p],
            free * disp_ref[2, p],
            force_ref[0, p] * sign,
            force_ref[1, p],
            force_ref[2, p],
            damage_ref[p],
            top * (free - flag),
        ]
        for f in range(fields):
            own[f, q] = here[f]
        values.append(here)

    sub = lax.broadcasted_iota(jnp.int32, (TILE, 128), 0)

    def spin(a, shift, axis):
        shift = shift % a.shape[axis]
        return pltpu.roll(a, shift, axis) if shift else a

    def spot(f, q):
        return 8 * (f % 4 // 2) + 2 * q + f % 2

    group = lax.broadcasted_iota(jnp.int32, (ly, 128), 1) // 8
    for j in range(packs):
        low = jnp.zeros((ly, 128), f32)
        high = jnp.zeros((ly, 128), f32)
        for f in range(4 * j, 4 * j + 4):
            for q in range(lx):
                k = spot(f, q)
                turned = spin(values[q][f], 8 * k + 8, 1)
                low = jnp.where(group == (k + 1) % 16, turned, low)
                high = jnp.where(group == k, turned, high)
        zsend[0, j] = low
        zsend[1, j] = high
    for j in range(pairs):
        fa, qa = divmod(2 * j, lx)
        fb, qb = divmod(2 * j + 1, lx)
        a, b = values[qa][fa], values[qb][fb]
        down_send[j] = jnp.where(sub < GHOST, a[0:TILE], spin(b[0:TILE], GHOST, 0))
        up_send[j] = jnp.where(sub < GHOST, spin(b[ly - TILE : ly], GHOST, 0), a[ly - TILE : ly])
    for e in range(extras):
        tile = jnp.zeros((TILE, 128), f32)
        for s in range(TILE):
            k, q = divmod(TILE * e + s, lx)
            tile = jnp.where(sub == s, spin(values[q][DEEP[k]][0:TILE], s - GHOST, 0), tile)
        down_send[pairs + e] = tile

    pl.semaphore_wait(barrier, number_near + 1)

    def remote(src, dst, send, recv, k, device):
        return pltpu.make_async_remote_copy(
            src_ref=src, dst_ref=dst, send_sem=send.at[k], recv_sem=recv.at[k],
            device_id=device, device_id_type=MESH,
        )

    def xcopy(src, dst, k):
        return remote(src, dst, xsend_sem, xrecv_sem, k, partner)

    corner_rows = {-1: (0, ly), 1: (ly - TILE, ly + TILE)}

    def halo(dy, dz):
        device = (gx, gy + dy, gz + dz)
        if dz == 0:
            if dy < 0:
                return remote(down_send, from_up, ysend_sem, yrecv_sem, 0, device)
            return remote(up_send, from_down, ysend_sem, yrecv_sem, 1, device)
        side = 0 if dz < 0 else 1
        if dy == 0:
            return remote(
                zsend.at[side], zrecv.at[side, :, 0:ly], zsend_sem, zrecv_sem, side, device
            )
        source, target = corner_rows[dy]
        return remote(
            zsend.at[side, :, source : source + TILE],
            zrecv.at[side, :, target : target + TILE],
            csend_sem, crecv_sem, 2 * side + (dy > 0), device,
        )

    order = [(0, -1), (0, 1), (-1, -1), (1, -1), (-1, 1), (1, 1), (-1, 0), (1, 0)]
    halos = {way: halo(*way) for way in order}
    x_own = xcopy(own, part, 0)
    x_own.start()
    for way in order:
        pl.when(there(*way))(halos[way].start)
    for dy, dz in order[:6]:
        pl.when(there(-dy, -dz))(halos[dy, dz].wait_recv)
    x_z = xcopy(zrecv, zpart, 1)
    x_z.start()
    pl.when(there(1, 0))(halos[-1, 0].wait_recv)
    x_up = xcopy(from_up, part_up, 2)
    x_up.start()
    pl.when(there(-1, 0))(halos[1, 0].wait_recv)
    x_down = xcopy(from_down, part_down, 3)
    x_down.start()

    lane_w = lax.broadcasted_iota(jnp.int32, (wide, 128), 1)
    odd = lane_w // 8 % 2

    def merge(a):
        return jnp.concatenate(
            [a[0:ly], jnp.where(sub < GHOST, a[ly : ly + TILE], a[ly + TILE : wide])], axis=0
        )

    def both_sides(source, f):
        low, high = source[0, f // 4], source[1, f // 4]
        return jnp.where(odd == f % 2, high, low)

    halves = [spin(both_sides(zrecv, f), -8 * spot(f, 0), 1) for f in range(fields)]
    for exchange in (x_own, x_z, x_up, x_down):
        exchange.wait_recv()
    greet(hop_sem)
    for f in range(fields):
        far = both_sides(zpart, f)
        far = -far if f in TURNED else far
        whole = halves[f]
        for q in range(lx):
            at = nx - 1 - q
            whole = jnp.where(lane_w // 16 == at, spin(far, 8 * (2 * at - spot(f, q)), 1), whole)
        if f in DEEP:
            gz_wide[DEEP.index(f)] = whole
        if f not in (0, 1, 2):
            gz_rows[f - 3] = merge(whole)

    def pieces(f, q):
        mine = q < lx
        at = q if mine else nx - 1 - q
        j, half = divmod(f * lx + at, 2)
        above, below = (from_up, from_down) if mine else (part_up, part_down)
        main = own[f, at] if mine else part[f, at]
        return main, above, below, j, half, at, (not mine) and f in TURNED

    def load_wide(f, q):
        main, above, below, j, half, at, turn = pieces(f, q)
        a, b = above[j], below[j]
        if half:
            a, b = spin(a, GHOST, 0), spin(b, GHOST, 0)
        e, s = divmod(DEEP.index(f) * lx + at, TILE)
        a = jnp.where(sub == GHOST, spin(above[pairs + e], GHOST - s, 0), a)
        out = jnp.concatenate([main, a, b], axis=0)
        return -out if turn else out

    def load_rows(f, q):
        main, above, below, j, half, at, turn = pieces(f, q)
        a, b = above[j], below[j]
        ghost = spin(jnp.where(sub < GHOST, b, a), GHOST, 0) if half else jnp.where(sub < GHOST, a, b)
        out = jnp.concatenate([main, ghost], axis=0)
        return -out if turn else out

    row = lax.broadcasted_iota(jnp.int32, (rows, 128), 0)
    lane = lax.broadcasted_iota(jnp.int32, (rows, 128), 1)
    inside = lane % 16
    ypos = gy * ly + jnp.where(row < ly + GHOST, row, row - rows)
    zpos = gz * lz + lane
    zghost = gz * lz + jnp.where(inside < 8, inside - 8, inside + (lz - 8))

    def element_at(pos, count):
        return jnp.where((pos >= 0) & (pos <= count - 2), 1.0, 0.0)

    yvalid = element_at(ypos, ngy * ly)
    valid = yvalid * element_at(zpos, ngz * lz)
    gvalid = jnp.where(lane < 16 * (nx - 1), yvalid * element_at(zghost, ngz * lz), 0.0)

    def y_up(a):
        return pltpu.roll(a, a.shape[0] - 1, 0)

    def y_dn(a):
        return pltpu.roll(a, 1, 0)

    def lanes(a):
        return lane_w if a.shape[0] == wide else lane

    def z_up(a, ghost, p):
        return jnp.where(lanes(a) == 127, spin(ghost, 119 - 16 * p, 1), pltpu.roll(a, 127, 1))

    def z_up_take(acc, a, p):
        return jnp.where(lanes(a) == 16 * p + 7, spin(a, 16 * p + 7, 1), acc)

    def z_dn(a, ghost, p):
        return jnp.where(lanes(a) == 0, spin(ghost, 121 - 16 * p, 1), pltpu.roll(a, 1, 1))

    def z_dn_take(acc, a, p):
        return jnp.where(lanes(a) == 16 * p + 8, spin(a, 16 * p + 9, 1), acc)

    def plane_up(a):
        return pltpu.roll(a, 112, 1)

    def plane_dn(a):
        return pltpu.roll(a, 16, 1)

    blank = jnp.zeros((rows, 128), f32)
    zero = jnp.zeros((TILE, 128), f32)

    def half_back(ss, yd, zd, yz):
        s = (ss - yd) + y_dn(ss + yd)
        d = (zd - yz) + y_dn(zd + yz)
        return s - d, s + d

    def damage_sum(q):
        a = load_wide(6, q)
        s = a + z_up(a, gz_wide[3], q)
        return merge(s + y_up(s)), a

    def rigidity(low, high, mask):
        rest = 1.0 - (low + high) * 0.125
        return (rest * rest + RESIDUAL_STIFFNESS) * mask

    low, a = damage_sum(0)
    taken = z_up_take(pltpu.roll(gz_wide[3], 127, 1), a, 0)
    for q in range(nx - 1):
        high, a = damage_sum(q + 1)
        stiff[q] = rigidity(low, high, valid)
        taken = z_up_take(taken, a, q + 1)
        low = high
    taken = gz_wide[3] + taken
    taken = merge(taken + y_up(taken))
    stiff[GZ] = rigidity(taken, plane_up(taken), gvalid)
    stiff[nx - 1] = blank

    def gather_back(ref, planes, emit):
        ghost = ref[GZ]
        below = blank
        taken = pltpu.roll(ghost, 1, 1)
        for q in range(planes):
            a = ref[q]
            s = a + z_dn(a, ghost, q)
            here = s + y_dn(s)
            emit(q, below + here)
            below = here
            taken = z_dn_take(taken, a, q)
        s = ghost + taken
        s = s + y_dn(s)
        emit(GZ, s + plane_dn(s))

    def inv_emit(q, total):
        free = (gz_rows[4] if q == GZ else load_rows(7, q)) > 0.0
        inverse[q] = jnp.where(free, 1.0 / jnp.where(free, stiff_diag * total, 1.0), 0.0)

    gather_back(stiff, nx, inv_emit)

    def forward(u, near_u, keep):
        zs, zd = u + near_u, near_u - u
        a, b = keep(y_up(zs)), keep(y_up(zd))
        zs, zd = keep(zs), keep(zd)
        return zs + a, a - zs, zd + b, b - zd

    def same(a):
        return a

    def pass_one(load, planes, keep, height, with_ghost):
        for c in range(3):
            ghost = load(c, GZ)
            taken = pltpu.roll(ghost, 127, 1)
            for q in range(planes):
                u = load(c, q)
                out = forward(u, z_up(u, ghost, q), keep)
                for m in range(4):
                    modes[4 * c + m, q, 0:height] = out[m][0:height]
                if with_ghost:
                    taken = z_up_take(taken, u, q)
            if with_ghost:
                out = forward(ghost, taken, keep)
                for m in range(4):
                    modes[4 * c + m, GZ] = out[m]

    def sm(mode_a, comp_a, mode_b, comp_b):
        return float(stiff_modes[3 * mode_a + comp_a, 3 * mode_b + comp_b])

    k_lame = sm(4, 0, 2, 1)
    k_two = sm(4, 0, 4, 0) - k_lame
    k_shear = sm(2, 0, 2, 0)
    k_twist = sm(3, 0, 5, 1)
    k_bend = sm(3, 1, 3, 1)
    k_cross = sm(3, 1, 5, 0)
    k_last = sm(7, 0, 7, 0)

    def element(low, high, g, energy_at):
        S = [low[m] + high[m] if m % 4 else None for m in range(12)]
        D = [high[m] - low[m] for m in range(12)]
        xX, xXY, xXZ, xXYZ = D[0:4]
        yX, yXY, yXZ, yXYZ = D[4:8]
        zX, zXY, zXZ, zXYZ = D[8:12]
        _, xY, xZ, xYZ = S[0:4]
        _, yY, yZ, yYZ = S[4:8]
        _, zY, zZ, zYZ = S[8:12]
        div = xX + yY + zZ
        sxy, sxz, syz = xY + yX, xZ + zX, yZ + zY
        if energy_at is not None:
            trace = 0.25 * div
            tens = jnp.maximum(trace, 0.0)
            third = trace / 3.0
            ex, ey, ez = 0.25 * xX - third, 0.25 * yY - third, 0.25 * zZ - third
            dev = ex * ex + ey * ey + ez * ez
            she = (sxy * sxy + sxz * sxz + syz * syz) * 0.0625
            energy = 0.5 * BULK_MODULUS * tens * tens + LAME_MU * (dev + 0.5 * she)
            hist[energy_at] = jnp.where(g > 0.0, energy, 0.0)
        gl, g2, gs = k_lame * g, k_two * g, k_shear * g
        gt, gb, gc, g3 = k_twist * g, k_bend * g, k_cross * g, k_last * g
        pressure = gl * div
        fxX, fyY, fzZ = pressure + g2 * xX, pressure + g2 * yY, pressure + g2 * zZ
        txy, txz, tyz = gs * sxy, gs * sxz, gs * syz
        tw = xYZ + yXZ + zXY
        fxYZ, fyXZ, fzXY = gt * (xYZ + tw), gt * (yXZ + tw), gt * (zXY + tw)
        fyYZ, fxXZ = gb * yYZ + gc * xXZ, gb * xXZ + gc * yYZ
        fzYZ, fxXY = gb * zYZ + gc * xXY, gb * xXY + gc * zYZ
        fyXY, fzXZ = gb * yXY + gc * zXZ, gb * zXZ + gc * yXY
        FD = [
            fxX, fxXY, fxXZ, g3 * xXYZ,
            txy, fyXY, fyXZ, g3 * yXYZ,
            txz, fzXY, fzXZ, g3 * zXYZ,
        ]
        FS = [
            None, txy, txz, fxYZ,
            None, fyY, tyz, fyYZ,
            None, tyz, fzZ, fzYZ,
        ]
        lows = [(-FD[m]) if FS[m] is None else FS[m] - FD[m] for m in range(12)]
        highs = [FD[m] if FS[m] is None else FS[m] + FD[m] for m in range(12)]
        return lows, highs

    def element_pass(layers, energies, to_end):
        def step(chunk, carry):
            r = pl.ds(pl.multiple_of(chunk * TILE, TILE), TILE)
            low = [modes[m, 0, r, :] for m in range(12)]
            held = None
            for p in range(layers):
                high = [modes[m, p + 1, r, :] for m in range(12)]
                lows, highs = element(
                    low, high, stiff[p, r, :], (p, r, slice(None)) if p < energies else None
                )
                for m in range(12):
                    modes[m, p, r, :] = lows[m] + held[m] if p else lows[m]
                held, low = highs, high
            if to_end:
                for m in range(12):
                    modes[m, layers, r, :] = held[m]
            low = [modes[m, GZ, r, :] for m in range(12)]
            lows, highs = element(
                low, [plane_up(a) for a in low], stiff[GZ, r, :],
                (GZ, r, slice(None)) if energies else None,
            )
            for m in range(12):
                modes[m, GZ, r, :] = lows[m] + plane_dn(highs[m])
            return carry

        lax.fori_loop(0, rows // TILE, step, 0, unroll=True)

    def each_node(planes, emit, carry):
        ghosts = [half_back(*(modes[4 * c + m, GZ] for m in range(4))) for c in range(3)]
        taken = [pltpu.roll(g[1], 1, 1) for g in ghosts]
        for q in range(planes):
            got = []
            for c in range(3):
                near_w, far_w = half_back(*(modes[4 * c + m, q] for m in range(4)))
                got.append(near_w + z_dn(far_w, ghosts[c][1], q))
                taken[c] = z_dn_take(taken[c], far_w, q)
            carry = emit(q, got, carry)
        emit(GZ, [ghosts[c][0] + taken[c] for c in range(3)], carry)
        return carry

    def fold(a):
        total = a[0:TILE]
        for i in range(TILE, ly, TILE):
            total = total + a[i : i + TILE]
        return total

    nd, ng = DISP_ITERS, DMG_ITERS
    gram, vector = {}, {}

    def load_start(c, q):
        return gz_wide[c] if q == GZ else load_wide(c, q)

    pass_one(load_start, nx, merge, rows, True)
    element_pass(nx - 1, lx + ng, True)

    def start_emit(q, got, dot):
        inv = inverse[q]
        for c in range(3):
            force = gz_rows[c] if q == GZ else load_rows(3 + c, q)
            r = force - got[c]
            v = inv * r
            basis[c, q] = v
            if q < lx:
                resid[c, q] = r[0:ly]
                dot = dot + fold((v * r)[0:ly])
        return dot

    vector[0] = each_node(nx, start_emit, zero)

    def hist_emit(q, total):
        top = gz_rows[4] if q == GZ else load_rows(7, q)
        react[q] = jnp.maximum(jnp.abs(top), 0.125 * total)

    gather_back(hist, lx + ng, hist_emit)

    for k in range(nd - 1):
        planes = lx + nd - 1 - k
        pass_one(lambda c, q, k=k: basis[3 * k + c, q], planes + 1, same, rows, True)
        element_pass(planes, 0, False)

        def apply_emit(q, got, carry, k=k):
            carry = list(carry)
            inv = inverse[q] * (2.0 / SPECTRUM)
            for c in range(3):
                w = got[c]
                here = basis[3 * k + c, q]
                v = inv * w - here
                if k:
                    v = 2.0 * v - basis[3 * (k - 1) + c, q]
                basis[3 * (k + 1) + c, q] = v
                if q < lx:
                    wi, vi = w[0:ly], v[0:ly]
                    if k + 2 < nd:
                        images[3 * k + c, q] = wi
                    carry[0] = carry[0] + fold(here[0:ly] * wi)
                    carry[1] = carry[1] + fold(vi * resid[c, q])
                    carry[2] = carry[2] + fold(vi * wi)
                    for j in range(k):
                        carry[3 + j] = carry[3 + j] + fold(vi * images[3 * j + c, q])
            return tuple(carry)

        got = each_node(planes, apply_emit, (zero,) * (3 + k))
        gram[k, k], vector[k + 1], gram[k + 1, k] = got[:3]
        for j in range(k):
            gram[k + 1, j] = got[3 + j]

    def last_energy():
        pass_one(lambda c, q: basis[3 * (nd - 1) + c, q], lx + 1, same, ly, False)
        total, middle = zero, zero
        for chunk in range(ly // TILE):
            r = slice(TILE * chunk, TILE * chunk + TILE)
            low = [modes[m, 0, r, :] for m in range(12)]
            for p in range(lx):
                high = [modes[m, p + 1, r, :] for m in range(12)]
                S = [low[m] + high[m] if m % 4 else None for m in range(12)]
                D = [high[m] - low[m] for m in range(12)]
                xX, xXY, xXZ, xXYZ = D[0:4]
                yX, yXY, yXZ, yXYZ = D[4:8]
                zX, zXY, zXZ, zXYZ = D[8:12]
                _, xY, xZ, xYZ = S[0:4]
                _, yY, yZ, yYZ = S[4:8]
                _, zY, zZ, zYZ = S[8:12]
                div = xX + yY + zZ
                sxy, sxz, syz = xY + yX, xZ + zX, yZ + zY
                tw = xYZ + yXZ + zXY
                sum_two = xX * xX + yY * yY + zZ * zZ
                sum_shear = sxy * sxy + sxz * sxz + syz * syz
                sum_twist = xYZ * xYZ + yXZ * yXZ + zXY * zXY + tw * tw
                sum_bend = (yYZ * yYZ + xXZ * xXZ) + (zYZ * zYZ + xXY * xXY) + (yXY * yXY + zXZ * zXZ)
                sum_cross = yYZ * xXZ + zYZ * xXY + yXY * zXZ
                sum_last = xXYZ * xXYZ + yXYZ * yXYZ + zXYZ * zXYZ
                energy = (
                    (k_lame * (div * div) + k_two * sum_two)
                    + (k_shear * sum_shear + k_twist * sum_twist)
                    + (k_bend * sum_bend + (2.0 * k_cross) * sum_cross)
                    + k_last * sum_last
                ) * stiff[p, r, :]
                if p + 1 < lx:
                    total = total + energy
                else:
                    middle = middle + energy
                low = high
        return total + 0.5 * middle

    gram[nd - 1, nd - 1] = last_energy()

    cy = yvalid + element_at(ypos - 1, ngy * ly)
    cz = element_at(zpos, ngz * lz) + element_at(zpos - 1, ngz * lz)
    czg = element_at(zghost, ngz * lz) + element_at(zghost - 1, ngz * lz)
    cxg = jnp.where((lane < 16) | (lane >= 16 * (nx - 1)), 1.0, 2.0)
    node = jnp.where(cy * cz > 0.0, 1.0, 0.0)
    gnode = jnp.where(cy * czg > 0.0, 1.0, 0.0)
    diag_scale = laplace_diag * TOUGHNESS * LENGTH_SCALE
    lap_scale = TOUGHNESS * LENGTH_SCALE / 36.0

    def lines(d, after, before, count_z):
        s, n = after + before, count_z * d
        mass, slope = 2.0 * n + s, n - s
        s, n = y_up(mass) + y_dn(mass), cy * mass
        both = 2.0 * n + s
        mixed = (n - s) + (2.0 * (cy * slope) + (y_up(slope) + y_dn(slope)))
        return 2.0 * mixed + both, mixed - both

    def laplace_pass(load, planes, emit, carry, with_ghost):
        ghost = load(GZ)
        after = pltpu.roll(ghost, 127, 1)
        before = pltpu.roll(ghost, 1, 1)
        reach = planes + 1 if planes < nx else nx
        ahead = []
        for q in range(reach):
            d = load(q)
            ahead.append(lines(d, z_up(d, ghost, q), z_dn(d, ghost, q), cz))
            if with_ghost:
                after = z_up_take(after, d, q)
                before = z_dn_take(before, d, q)
            p = q - 1
            if p >= 0:
                total = ahead[p][0] if p == 0 else 2.0 * ahead[p][0] + ahead[p - 1][1]
                carry = emit(p, lap_scale * (total + ahead[q][1]), carry)
        if with_ghost:
            inner, outer = lines(ghost, after, before, czg)
            total = cxg * inner + jnp.where(lane >= 16, plane_dn(outer), 0.0)
            total = total + jnp.where(lane < 16 * (nx - 1), plane_up(outer), 0.0)
            emit(GZ, lap_scale * total, carry)
        return carry

    def reaction_of(q):
        return TOUGHNESS / LENGTH_SCALE + 2.0 * react[q]

    def old_damage(q):
        return gz_rows[3] if q == GZ else load_rows(6, q)

    def dstart(q, lap, dot):
        reaction = reaction_of(q)
        if q == GZ:
            count, mask = cxg * cy * czg, gnode
        else:
            count, mask = (cy * cz if q == 0 else 2.0 * cy * cz), node
        inv = mask / (diag_scale * count + reaction)
        dinverse[q] = inv
        r = 2.0 * react[q] - (lap + reaction * old_damage(q))
        v = inv * r
        dbasis[0, q] = v
        if q < lx:
            dresid[q] = r[0:ly]
            dot = dot + fold((v * r)[0:ly])
        return dot

    dvector, dgram = {}, {}
    dvector[0] = laplace_pass(old_damage, lx + ng, dstart, zero, True)
    dimages = {}
    for k in range(ng):
        more = k + 1 < ng

        def dstep(q, lap, carry, k=k, more=more):
            carry = list(carry)
            here = dbasis[k, q]
            w = lap + reaction_of(q) * here
            if q < lx:
                carry[0] = carry[0] + fold((here * w)[0:ly])
            if more:
                v = dinverse[q] * w - here
                if k:
                    v = 2.0 * v - dbasis[k - 1, q]
                dbasis[k + 1, q] = v
                if q < lx:
                    carry[1] = carry[1] + fold(v[0:ly] * dresid[q])
                    carry[2] = carry[2] + fold((v * w)[0:ly])
            return tuple(carry)

        got = laplace_pass(
            lambda q, k=k: dbasis[k, q], lx + ng - 1 - k, dstep, (zero,) * (3 if more else 1), more
        )
        dgram[k, k] = got[0]
        if more:
            dvector[k + 1], dgram[k + 1, k] = got[1:]

    parts = [vector[i] for i in range(nd)] + [dvector[i] for i in range(ng)]
    parts += [gram[i, j] for i in range(nd) for j in range(i + 1)]
    parts += [dgram[i, j] for i in range(ng) for j in range(i + 1)]
    at = lax.broadcasted_iota(jnp.int32, (1, 128), 1)
    packed = jnp.zeros((1, 128), f32)
    for i, piece in enumerate(parts):
        line = jnp.sum(piece, axis=0, keepdims=True)
        packed = jnp.where(at == i, jnp.sum(line, axis=1, keepdims=True), packed)
    mine = gx * npeer + me
    sums[mine] = packed
    pl.semaphore_wait(hop_sem, number_near)

    def peer_copy(side, o, slot):
        q = lax.rem(me + o, npeer)
        k = side * npeer + o
        return remote(
            sums.at[mine], sums.at[slot], asend_sem, arecv_sem, k,
            (gx if side == 0 else 1 - gx, q // ngz, lax.rem(q, ngz)),
        )

    peers = [(side, o) for o in range(npeer) for side in (0, 1) if side or o]
    sends = [peer_copy(side, o, mine) for side, o in peers]
    for s in sends:
        s.start()
    for q in range(lx):
        out_history[place(q)] = react[q, 0:ly]
    for side, o in peers:
        from_x = gx if side == 0 else 1 - gx
        peer_copy(side, o, from_x * npeer + lax.rem(me + npeer - o, npeer)).wait_recv()
    layer = [sums[i] for i in range(2 * npeer)]
    while len(layer) > 1:
        layer = [a + b for a, b in zip(layer[::2], layer[1::2])] + layer[len(layer) & ~1 :]
    whole = layer[0]

    scalars = [
        jnp.sum(jnp.where(at == i, whole, 0.0), axis=1, keepdims=True) for i in range(len(parts))
    ]

    def solve(rhs, lower):
        n = len(rhs)
        A = [[lower[max(i, j)][min(i, j)] for j in range(n)] for i in range(n)]
        b = list(rhs)
        for i in range(n):
            pivot = 1.0 / A[i][i]
            for r in range(i + 1, n):
                ratio = A[r][i] * pivot
                for c in range(i + 1, n):
                    A[r][c] = A[r][c] - ratio * A[i][c]
                b[r] = b[r] - ratio * b[i]
        out = [None] * n
        for i in reversed(range(n)):
            s = b[i]
            for j in range(i + 1, n):
                s = s - A[i][j] * out[j]
            out[i] = s / A[i][i]
        return out

    def triangle(flat, n):
        return [[flat[k * (k + 1) // 2 + j] for j in range(k + 1)] for k in range(n)]

    rest = scalars[nd + ng :]
    cut = nd * (nd + 1) // 2
    weights = solve(scalars[:nd], triangle(rest[:cut], nd))
    dweights = solve(scalars[nd : nd + ng], triangle(rest[cut:], ng))
    for q in range(lx):
        p = place(q)
        for c in range(3):
            x = own[c, q]
            for k in range(nd):
                x = x + weights[k] * basis[3 * k + c, q, 0:ly]
            out_disp[c, p] = sign * x if c == 0 else x
        d = own[6, q]
        for k in range(ng):
            d = d + dweights[k] * dbasis[k, q, 0:ly]
        out_damage[p] = d

    for way in order:
        pl.when(there(*way))(halos[way].wait_send)
    for exchange in (x_own, x_z, x_up, x_down):
        exchange.wait_send()
    for s in sends:
        s.wait_send()


def hand_on(*refs):
    for source, target in zip(refs[:3], refs[3:]):
        target[...] = source[...]


def body_fused(sizes, *arrays):
    ngy, ngz, lx, ly, lz = sizes
    nx, rows, wide, fields = 2 * lx, ly + TILE, ly + 2 * TILE, 8
    packs, pairs, extras = fields * lx // 16, fields * lx // 2, len(DEEP) * lx // TILE
    npeer = ngy * ngz
    f32 = jnp.float32
    planes = (nx + 1, rows, lz)
    vmem = pl.BlockSpec(memory_space=pltpu.VMEM)
    hbm = pl.BlockSpec(memory_space=pltpu.HBM)
    dma = pltpu.SemaphoreType.DMA

    def room(*shape):
        return pltpu.VMEM(shape, f32)

    results = pl.pallas_call(
        functools.partial(kernel, sizes),
        out_shape=(
            jax.ShapeDtypeStruct((3, lx, ly, lz), f32),
            jax.ShapeDtypeStruct((lx, ly, lz), f32),
            jax.ShapeDtypeStruct((lx, ly, lz), f32),
        ),
        in_specs=[hbm] * 6,
        out_specs=(vmem,) * 3,
        scratch_shapes=[
            room(3, lx, ly, lz),
            room(3, lx, ly, lz),
            room(lx, ly, lz),
            room(lx, ly, lz),
            pltpu.VMEM((lx, ly, lz), jnp.int32),
            pltpu.VMEM((lx, ly, lz), jnp.int32),
            room(fields, lx, ly, lz),
            room(fields, lx, ly, lz),
            room(pairs + extras, TILE, 128),
            room(pairs, TILE, 128),
            room(pairs + extras, TILE, 128),
            room(pairs, TILE, 128),
            room(pairs + extras, TILE, 128),
            room(pairs, TILE, 128),
            room(2, packs, ly, 128),
            room(2, packs, wide, 128),
            room(2, packs, wide, 128),
            room(4, wide, 128),
            room(5, rows, 128),
            room(12, *planes),
            room(3 * DISP_ITERS, *planes),
            room(3 * (DISP_ITERS - 2), lx, ly, lz),
            room(3, lx, ly, lz),
            room(*planes),
            room(*planes),
            room(*planes),
            room(*planes),
            room(*planes),
            room(DMG_ITERS, *planes),
            room(lx, ly, lz),
            room(2 * npeer, 1, 128),
            dma((6,)),
            dma((2,)),
            dma((2,)),
            dma((2,)),
            dma((2,)),
            dma((4,)),
            dma((4,)),
            dma((4,)),
            dma((4,)),
            dma((2 * npeer,)),
            dma((2 * npeer,)),
            pltpu.SemaphoreType.REGULAR,
        ],
        compiler_params=pltpu.CompilerParams(
            collective_id=0, has_side_effects=True, vmem_limit_bytes=VMEM_LIMIT
        ),
    )(*arrays)
    return pl.pallas_call(
        hand_on,
        out_shape=tuple(jax.ShapeDtypeStruct(r.shape, f32) for r in results),
        in_specs=[vmem] * 3,
        out_specs=(vmem,) * 3,
    )(*results)


VMEM_LIMIT = 60 * 1024 * 1024


def solution(mesh):
    shape = dict(mesh.shape)

    def body(*arrays):
        lx, ly, lz = arrays[2].shape
        fits = shape["gx"] == 2 and shape["gy"] * shape["gz"] > 1
        fits = fits and max(shape["gy"], shape["gz"]) <= 4
        fits = fits and lx == 4 and ly % 8 == 0 and lz == 128
        if fits:
            return body_fused((shape["gy"], shape["gz"], lx, ly, lz), *arrays)
        return body_any_mesh(*arrays)

    return jax.shard_map(
        body,
        mesh=mesh,
        in_specs=(
            P(None, "gx", "gy", "gz"),
            P(None, "gx", "gy", "gz"),
            P("gx", "gy", "gz"),
            P("gx", "gy", "gz"),
            P("gx", "gy", "gz"),
            P("gx", "gy", "gz"),
        ),
        out_specs=(P(None, "gx", "gy", "gz"), P("gx", "gy", "gz"), P("gx", "gy", "gz")),
        check_vma=False,
    )
```

time: 34.9 us -> 25.1 us (0.72)
  Pallas kernels: 34.1 us -> 24.3 us
    pallas_call x1, Pallas kernels: 32.5 us -> 22.7 us  [body_fused(): pl.pallas_call(functools.partial(kernel, sizes), out_shape=(jax.ShapeDtyp...]
where the time goes in v1:
time: 25.1 us; the launch traced here: 24.9 us
  Pallas kernels  24.3 us (97%)
  between operations  0.64 us (3%)
    pallas_call x1, Pallas kernels, body_fused(): pl.pallas_call(functools.partial(kernel, sizes), out_shape=(jax.ShapeDtyp...  22.7 us
    pallas_call x1, Pallas kernels, body_fused(): pl.pallas_call(hand_on, out_shape=tuple((jax.ShapeDtypeStruct(r.shape, f3...  1.58 us

profile of v1, /device:TPU:0, one launch (start us, length us, event | category | flops | bytes accessed | tf_op | source)
XLA Modules:
  0.0 24.9 jit_solution(3953163435778500715)
XLA Ops:
  0.6 22.7 %shard_map.85 = (f32[3,4,16,128]{3,2,1,0:T(8,128)}, f32[4,16,128]{2,1,0:T(8,128)}, f32[4,16,128]{2,1,0:T(8,128)}) custom-call(f32[3,4,16,128]{3,2,1,0:T(8,128)} %disp_in.1, f32[3,4,16,128]{3,2,1,0:T(8,128)} %force_in.1, f32[4,16,128]{2,1,0:T(8,128)} %damage_in.1, f32[4,16,128]{2,1,0:T(8,128)} %history_in.1, s32[4,16,128]{2,1,0:T(8,128)} %labels_in.1, ...), custom_call_target="tpu_custom_call" | custom-call | tf_op jit(solution)/shard_map/pallas_call | solution.py:1101
  23.4 1.6 %shard_map.86 = (f32[3,4,16,128]{3,2,1,0:T(8,128)}, f32[4,16,128]{2,1,0:T(8,128)}, f32[4,16,128]{2,1,0:T(8,128)}) custom-call(f32[3,4,16,128]{3,2,1,0:T(8,128)} %get-tuple-element.6.refs_0_, f32[4,16,128]{2,1,0:T(8,128)} %get-tuple-element.7.refs_1_, f32[4,16,128]{2,1,0:T(8,128)} %get-tuple-element.8.refs_2_), custom_call_target="tpu_custom_call" | custom-call | tf_op jit(solution)/shard_map/pallas_call | solution.py:1159

commit v2 on v1

--- a/solution.py
+++ b/solution.py
@@ -1080,8 +1080,15 @@
 
 
 def hand_on(*refs):
-    for source, target in zip(refs[:3], refs[3:]):
-        target[...] = source[...]
+    sources, targets, sem = refs[:3], refs[3:6], refs[6]
+    copies = [
+        pltpu.make_async_copy(source, target, sem.at[i])
+        for i, (source, target) in enumerate(zip(sources, targets))
+    ]
+    for copy in copies:
+        copy.start()
+    for copy in copies:
+        copy.wait()
 
 
 def body_fused(sizes, *arrays):
@@ -1101,9 +1108,9 @@
     results = pl.pallas_call(
         functools.partial(kernel, sizes),
         out_shape=(
-            jax.ShapeDtypeStruct((3, lx, ly, lz), f32),
-            jax.ShapeDtypeStruct((lx, ly, lz), f32),
-            jax.ShapeDtypeStruct((lx, ly, lz), f32),
+            pltpu.VMEM((3, lx, ly, lz), f32),
+            pltpu.VMEM((lx, ly, lz), f32),
+            pltpu.VMEM((lx, ly, lz), f32),
         ),
         in_specs=[hbm] * 6,
         out_specs=(vmem,) * 3,
@@ -1155,16 +1162,18 @@
         compiler_params=pltpu.CompilerParams(
             collective_id=0, has_side_effects=True, vmem_limit_bytes=VMEM_LIMIT
         ),
-    )(*arrays)
+    )(*[pltpu.with_memory_space_constraint(a, pltpu.HBM) for a in arrays])
     return pl.pallas_call(
         hand_on,
         out_shape=tuple(jax.ShapeDtypeStruct(r.shape, f32) for r in results),
         in_specs=[vmem] * 3,
-        out_specs=(vmem,) * 3,
-    )(*results)
-
-
-VMEM_LIMIT = 60 * 1024 * 1024
+        out_specs=(hbm,) * 3,
+        scratch_shapes=[dma((3,))],
+        compiler_params=pltpu.CompilerParams(vmem_limit_bytes=1024 * 1024),
+    )(*[pltpu.with_memory_space_constraint(r, pltpu.VMEM) for r in results])
+
+
+VMEM_LIMIT = 24 * 1024 * 1024
 
 
 def solution(mesh):

time: 25.1 us -> 23.6 us (0.940)
  Pallas kernels: 24.3 us -> 22.8 us
    pallas_call x1, Pallas kernels: 1.58 us -> 0.69 us  [body_fused(): pl.pallas_call(hand_on, out_shape=tuple((jax.ShapeDtypeStruct(r.shape, f3...]
    pallas_call x1, Pallas kernels: 22.7 us -> 22.1 us  [body_fused(): pl.pallas_call(functools.partial(kernel, sizes), out_shape=(pltpu.VMEM((3...]
where the time goes in v2:
time: 23.6 us; the launch traced here: 23.4 us
  Pallas kernels  22.8 us (97%)
  between operations  0.64 us (3%)
    pallas_call x1, Pallas kernels, body_fused(): pl.pallas_call(functools.partial(kernel, sizes), out_shape=(pltpu.VMEM((3...  22.1 us
    pallas_call x1, Pallas kernels, body_fused(): pl.pallas_call(hand_on, out_shape=tuple((jax.ShapeDtypeStruct(r.shape, f3...  0.69 us

profile of v2, /device:TPU:0, one launch (start us, length us, event | category | flops | bytes accessed | tf_op | source)
XLA Modules:
  0.0 23.4 jit_solution(14078260012550751837)
XLA Ops:
  0.6 22.1 %shard_map.85 = (f32[3,4,16,128]{3,2,1,0:T(8,128)S(1)}, f32[4,16,128]{2,1,0:T(8,128)S(1)}, f32[4,16,128]{2,1,0:T(8,128)S(1)}) custom-call(f32[3,4,16,128]{3,2,1,0:T(8,128)} %disp_in.1, f32[3,4,16,128]{3,2,1,0:T(8,128)} %force_in.1, f32[4,16,128]{2,1,0:T(8,128)} %damage_in.1, f32[4,16,128]{2,1,0:T(8,128)} %history_in.1, s32[4,16,128]{2,1,0:T(8,128)} %labels_in.1, ...), custom_call_target="tpu_custom_call" | custom-call | tf_op jit(solution)/shard_map/pallas_call | solution.py:1108
  22.7 0.7 %shard_map.86 = (f32[3,4,16,128]{3,2,1,0:T(8,128)}, f32[4,16,128]{2,1,0:T(8,128)}, f32[4,16,128]{2,1,0:T(8,128)}) custom-call(f32[3,4,16,128]{3,2,1,0:T(8,128)S(1)} %get-tuple-element.6.refs_0_, f32[4,16,128]{2,1,0:T(8,128)S(1)} %get-tuple-element.7.refs_1_, f32[4,16,128]{2,1,0:T(8,128)S(1)} %get-tuple-element.8.refs_2_), custom_call_target="tpu_custom_call" | custom-call | tf_op jit(solution)/shard_map/pallas_call | solution.py:1166

commit v3 on v2

--- a/solution.py
+++ b/solution.py
@@ -284,8 +284,7 @@
 SPECTRUM = 3.2
 TILE = 8
 GHOST = 4
-DEEP = (0, 1, 2, 6)
-TURNED = (0, 3)
+DEEP = 4
 MESH = pl.DeviceIdType.MESH
 
 
@@ -319,17 +318,18 @@
     history_ref,
     labels_ref,
     flags_ref,
-    own,
-    part,
-    down_send,
-    up_send,
-    from_up,
-    from_down,
-    part_up,
-    part_down,
-    zsend,
-    zrecv,
-    zpart,
+    full_deep,
+    full_flat,
+    down_deep,
+    up_deep,
+    down_flat,
+    up_flat,
+    ghost_deep,
+    ghost_flat,
+    zsend_deep,
+    zsend_flat,
+    zbuf_deep,
+    zbuf_flat,
     gz_wide,
     gz_rows,
     modes,
@@ -343,6 +343,9 @@
     dinverse,
     dbasis,
     dresid,
+    basis_part,
+    dbasis_part,
+    react_part,
     sums,
     in_sem,
     ysend_sem,
@@ -361,23 +364,28 @@
     nx = 2 * lx
     fields = 8
     npeer = ngy * ngz
-    pairs = fields * lx // 2
+    pairs = DEEP * lx // 2
     packs = fields * lx // 16
-    extras = len(DEEP) * lx // TILE
-    wide, rows = ly + 2 * TILE, ly + TILE
+    extras = DEEP * lx // TILE
+    wide, rows = 3 * TILE, 2 * TILE
     GZ = nx
     f32 = jnp.float32
     stiff_modes, stiff_diag, laplace_diag = walsh_tables()
     gx, gy, gz = lax.axis_index("gx"), lax.axis_index("gy"), lax.axis_index("gz")
     me = gy * ngz + gz
     partner = (1 - gx, gy, gz)
+    outward = 2 * gx - 1
+    full, zsend, zbuf = (full_deep, full_flat), (zsend_deep, zsend_flat), (zbuf_deep, zbuf_flat)
 
     def there(dy, dz):
         y, z = gy + dy, gz + dz
         return (y >= 0) & (y < ngy) & (z >= 0) & (z < ngz)
 
+    def device(core, dy, dz):
+        return core, lax.rem(gy + dy + ngy, ngy), lax.rem(gz + dz + ngz, ngz)
+
     near = [(dy, dz) for dy in (-1, 0, 1) for dz in (-1, 0, 1) if dy or dz]
-    number_near = sum(there(dy, dz).astype(jnp.int32) for dy, dz in near)
+    number_near = 2 * sum(there(dy, dz).astype(jnp.int32) for dy, dz in near)
 
     barrier = pltpu.get_barrier_semaphore()
 
@@ -386,9 +394,10 @@
 
             @pl.when(there(dy, dz))
             def _():
-                pl.semaphore_signal(
-                    semaphore, inc=1, device_id=(gx, gy + dy, gz + dz), device_id_type=MESH
-                )
+                for core in (gx, 1 - gx):
+                    pl.semaphore_signal(
+                        semaphore, inc=1, device_id=device(core, dy, dz), device_id_type=MESH
+                    )
 
     greet(barrier)
     pl.semaphore_signal(barrier, inc=1, device_id=partner, device_id_type=MESH)
@@ -409,47 +418,39 @@
     for load in loads:
         load.start()
 
+    zero = jnp.zeros((TILE, 128), f32)
     for dz, side in ((1, 0), (-1, 1)):
-        for dy, low, high in ((0, 0, ly), (1, ly, ly + TILE), (-1, ly + TILE, wide)):
-
-            @pl.when(jnp.logical_not(there(dy, dz)))
-            def _():
-                zrecv[side, :, low:high] = jnp.zeros((packs, high - low, 128), f32)
-
-    @pl.when(jnp.logical_not(there(1, 0)))
+
+        @pl.when(jnp.logical_not(there(0, dz)))
+        def _():
+            for core in range(2):
+                for ref in zbuf:
+                    ref[core, side, 0:2] = jnp.zeros((2, TILE, 128), f32)
+
+        @pl.when(jnp.logical_not(there(outward, dz)))
+        def _():
+            for core in range(2):
+                for ref in zbuf:
+                    ref[core, side, 2] = zero
+
+    @pl.when(jnp.logical_not(there(outward, 0)))
     def _():
-        from_up[...] = jnp.zeros(from_up.shape, f32)
-
-    @pl.when(jnp.logical_not(there(-1, 0)))
-    def _():
-        from_down[...] = jnp.zeros(from_down.shape, f32)
+        ghost_deep[...] = jnp.zeros(ghost_deep.shape, f32)
+        ghost_flat[...] = jnp.zeros(ghost_flat.shape, f32)
 
     for load in loads:
         load.wait()
 
-    sign = (1 - 2 * gx).astype(f32)
-
-    def place(q):
-        return q + gx * (lx - 1 - 2 * q)
-
     values = []
-    for q in range(lx):
-        p = place(q)
+    for p in range(lx):
         flag = flags_ref[p].astype(f32)
         free = 1.0 - flag
         top = jnp.maximum(history_ref[p], CRACK_HISTORY * labels_ref[p].astype(f32))
-        here = [
-            free * disp_ref[0, p] * sign,
-            free * disp_ref[1, p],
-            free * disp_ref[2, p],
-            force_ref[0, p] * sign,
-            force_ref[1, p],
-            force_ref[2, p],
-            damage_ref[p],
-            top * (free - flag),
-        ]
+        here = [free * disp_ref[c, p] for c in range(3)]
+        here += [damage_ref[p]] + [force_ref[c, p] for c in range(3)] + [top * (free - flag)]
         for f in range(fields):
-            own[f, q] = here[f]
+            for half in range(2):
+                full[f // DEEP][f % DEEP, half, gx * lx + p] = here[f][TILE * half : TILE * half + TILE]
         values.append(here)
 
     sub = lax.broadcasted_iota(jnp.int32, (TILE, 128), 0)
@@ -471,126 +472,156 @@
                 turned = spin(values[q][f], 8 * k + 8, 1)
                 low = jnp.where(group == (k + 1) % 16, turned, low)
                 high = jnp.where(group == k, turned, high)
-        zsend[0, j] = low
-        zsend[1, j] = high
-    for j in range(pairs):
-        fa, qa = divmod(2 * j, lx)
-        fb, qb = divmod(2 * j + 1, lx)
-        a, b = values[qa][fa], values[qb][fb]
-        down_send[j] = jnp.where(sub < GHOST, a[0:TILE], spin(b[0:TILE], GHOST, 0))
-        up_send[j] = jnp.where(sub < GHOST, spin(b[ly - TILE : ly], GHOST, 0), a[ly - TILE : ly])
+        for half in range(2):
+            zsend[j][0, half] = low[TILE * half : TILE * half + TILE]
+            zsend[j][1, half] = high[TILE * half : TILE * half + TILE]
+    for first, down, up in ((0, down_deep, up_deep), (DEEP, down_flat, up_flat)):
+        for j in range(pairs):
+            fa, qa = divmod(2 * j, lx)
+            fb, qb = divmod(2 * j + 1, lx)
+            a, b = values[qa][first + fa], values[qb][first + fb]
+            down[j] = jnp.where(sub < GHOST, a[0:TILE], spin(b[0:TILE], GHOST, 0))
+            up[j] = jnp.where(sub < GHOST, spin(b[ly - TILE : ly], GHOST, 0), a[ly - TILE : ly])
     for e in range(extras):
         tile = jnp.zeros((TILE, 128), f32)
         for s in range(TILE):
-            k, q = divmod(TILE * e + s, lx)
-            tile = jnp.where(sub == s, spin(values[q][DEEP[k]][0:TILE], s - GHOST, 0), tile)
-        down_send[pairs + e] = tile
+            f, q = divmod(TILE * e + s, lx)
+            tile = jnp.where(sub == s, spin(values[q][f][0:TILE], s - GHOST, 0), tile)
+        down_deep[pairs + e] = tile
 
     pl.semaphore_wait(barrier, number_near + 1)
 
-    def remote(src, dst, send, recv, k, device):
+    def remote(src, dst, send, recv, target):
         return pltpu.make_async_remote_copy(
-            src_ref=src, dst_ref=dst, send_sem=send.at[k], recv_sem=recv.at[k],
-            device_id=device, device_id_type=MESH,
+            src_ref=src, dst_ref=dst, send_sem=send, recv_sem=recv,
+            device_id=target, device_id_type=MESH,
         )
 
     def xcopy(src, dst, k):
-        return remote(src, dst, xsend_sem, xrecv_sem, k, partner)
-
-    corner_rows = {-1: (0, ly), 1: (ly - TILE, ly + TILE)}
-
-    def halo(dy, dz):
-        device = (gx, gy + dy, gz + dz)
-        if dz == 0:
-            if dy < 0:
-                return remote(down_send, from_up, ysend_sem, yrecv_sem, 0, device)
-            return remote(up_send, from_down, ysend_sem, yrecv_sem, 1, device)
+        return remote(src, dst, xsend_sem.at[k], xrecv_sem.at[k], partner)
+
+    def zcopy(source, dz, pack, core):
         side = 0 if dz < 0 else 1
-        if dy == 0:
-            return remote(
-                zsend.at[side], zrecv.at[side, :, 0:ly], zsend_sem, zrecv_sem, side, device
-            )
-        source, target = corner_rows[dy]
         return remote(
-            zsend.at[side, :, source : source + TILE],
-            zrecv.at[side, :, target : target + TILE],
-            csend_sem, crecv_sem, 2 * side + (dy > 0), device,
+            zsend[pack].at[side], zbuf[pack].at[source, side, 0:2],
+            zsend_sem.at[4 * core + 2 * side + pack], zrecv_sem.at[4 * source + 2 * side + pack],
+            device(core, 0, dz),
         )
 
-    order = [(0, -1), (0, 1), (-1, -1), (1, -1), (-1, 1), (1, 1), (-1, 0), (1, 0)]
-    halos = {way: halo(*way) for way in order}
-    x_own = xcopy(own, part, 0)
-    x_own.start()
-    for way in order:
-        pl.when(there(*way))(halos[way].start)
-    for dy, dz in order[:6]:
-        pl.when(there(-dy, -dz))(halos[dy, dz].wait_recv)
-    x_z = xcopy(zrecv, zpart, 1)
-    x_z.start()
-    pl.when(there(1, 0))(halos[-1, 0].wait_recv)
-    x_up = xcopy(from_up, part_up, 2)
-    x_up.start()
-    pl.when(there(-1, 0))(halos[1, 0].wait_recv)
-    x_down = xcopy(from_down, part_down, 3)
-    x_down.start()
+    def corner(source, dy, dz, pack):
+        side = 0 if dz < 0 else 1
+        return remote(
+            zsend[pack].at[side, int(dy > 0)], zbuf[pack].at[source, side, 2],
+            csend_sem.at[4 * (dy > 0) + 2 * side + pack],
+            crecv_sem.at[4 * source + 2 * side + pack],
+            device(int(dy < 0), dy, dz),
+        )
+
+    def ycopy(source, dy, flat):
+        if flat:
+            src, dst = (down_flat if dy < 0 else up_flat), ghost_flat.at[source]
+        elif dy < 0:
+            src, dst = down_deep, ghost_deep.at[source]
+        else:
+            src, dst = up_deep, ghost_deep.at[source, 0:pairs]
+        return remote(
+            src, dst, ysend_sem.at[2 * flat + (dy > 0)], yrecv_sem.at[2 * flat + source],
+            device(int(dy < 0), dy, 0),
+        )
+
+    own = pl.ds(gx * lx, lx)
+    x_own = [
+        xcopy(full[flat].at[:, :, own], full[flat].at[:, :, own], flat) for flat in range(2)
+    ]
+    halos = [[], []]
+    for flat in (0, 1):
+        for source in (0, 1):
+            ways = [((dy, dz), corner(source, dy, dz, flat)) for dy in (-1, 1) for dz in (-1, 1)]
+            ways += [((dy, 0), ycopy(source, dy, flat)) for dy in (-1, 1)]
+            ways += [((0, dz), zcopy(source, dz, flat, core)) for dz in (-1, 1) for core in (0, 1)]
+            halos[flat] += [((gx == source) & there(*way), copy) for way, copy in ways]
+    for flat in (0, 1):
+        x_own[flat].start()
+        for guard, copy in halos[flat]:
+            pl.when(guard)(copy.start)
+
+    def arrive(flat):
+        for dz in (-1, 1):
+            for source in range(2):
+                pl.when(there(0, -dz))(zcopy(source, dz, flat, 0).wait_recv)
+        x_own[flat].wait_recv()
+        for dz in (-1, 1):
+            for source in range(2):
+                pl.when(there(outward, -dz))(corner(source, 1, dz, flat).wait_recv)
+        for core in range(2):
+            for source in range(2):
+                pl.when((gx == core) & there(outward, 0))(
+                    ycopy(source, -1 if core else 1, flat).wait_recv
+                )
+
+    arrive(0)
 
     lane_w = lax.broadcasted_iota(jnp.int32, (wide, 128), 1)
     odd = lane_w // 8 % 2
 
     def merge(a):
         return jnp.concatenate(
-            [a[0:ly], jnp.where(sub < GHOST, a[ly : ly + TILE], a[ly + TILE : wide])], axis=0
+            [a[0:TILE], jnp.where(sub < GHOST, a[TILE : 2 * TILE], a[2 * TILE :])], axis=0
         )
 
-    def both_sides(source, f):
-        low, high = source[0, f // 4], source[1, f // 4]
-        return jnp.where(odd == f % 2, high, low)
-
-    halves = [spin(both_sides(zrecv, f), -8 * spot(f, 0), 1) for f in range(fields)]
-    for exchange in (x_own, x_z, x_up, x_down):
-        exchange.wait_recv()
-    greet(hop_sem)
-    for f in range(fields):
-        far = both_sides(zpart, f)
-        far = -far if f in TURNED else far
-        whole = halves[f]
-        for q in range(lx):
-            at = nx - 1 - q
-            whole = jnp.where(lane_w // 16 == at, spin(far, 8 * (2 * at - spot(f, q)), 1), whole)
-        if f in DEEP:
-            gz_wide[DEEP.index(f)] = whole
-        if f not in (0, 1, 2):
-            gz_rows[f - 3] = merge(whole)
+    is_lower = sub + TILE * gx < TILE
+    from_theirs = (sub + GHOST * gx) % TILE < GHOST
+
+    def order(lower, upper):
+        return jnp.where(is_lower, lower, upper), jnp.where(is_lower, upper, lower)
+
+    def ghost_tiles(f):
+        halves = []
+        for source in range(2):
+            ref = zbuf[f // 4]
+            low, high = (
+                jnp.concatenate([ref[source, side, k] for k in range(3)], axis=0) for side in range(2)
+            )
+            both = jnp.where(odd == f % 2, high, low)
+            halves.append(spin(both, 8 * (2 * lx * source - spot(f, 0)), 1))
+        whole = jnp.where(lane_w < 16 * lx, *halves)
+        return *order(whole[0:TILE], whole[TILE : 2 * TILE]), whole[2 * TILE :]
+
+    def line_wide(tile, other, up, down):
+        return jnp.concatenate(
+            [tile, jnp.where(is_lower, other, up), jnp.where(is_lower, down, other)], axis=0
+        )
+
+    def line_rows(tile, other, ghost):
+        return jnp.concatenate([tile, jnp.where(from_theirs, other, ghost)], axis=0)
+
+    for f in range(DEEP):
+        tile, other, ghost = ghost_tiles(f)
+        gz_wide[f] = line_wide(tile, other, ghost, ghost)
+    gz_rows[0] = merge(gz_wide[DEEP - 1])
 
     def pieces(f, q):
-        mine = q < lx
-        at = q if mine else nx - 1 - q
-        j, half = divmod(f * lx + at, 2)
-        above, below = (from_up, from_down) if mine else (part_up, part_down)
-        main = own[f, at] if mine else part[f, at]
-        return main, above, below, j, half, at, (not mine) and f in TURNED
+        source, p = divmod(q, lx)
+        j, half = divmod(f % DEEP * lx + p, 2)
+        ghost = ghost_deep[source, j] if f < DEEP else ghost_flat[source, j]
+        ref = full[f // DEEP]
+        return *order(ref[f % DEEP, 0, q], ref[f % DEEP, 1, q]), spin(ghost, GHOST * half, 0)
 
     def load_wide(f, q):
-        main, above, below, j, half, at, turn = pieces(f, q)
-        a, b = above[j], below[j]
-        if half:
-            a, b = spin(a, GHOST, 0), spin(b, GHOST, 0)
-        e, s = divmod(DEEP.index(f) * lx + at, TILE)
-        a = jnp.where(sub == GHOST, spin(above[pairs + e], GHOST - s, 0), a)
-        out = jnp.concatenate([main, a, b], axis=0)
-        return -out if turn else out
+        tile, other, ghost = pieces(f, q)
+        e, s = divmod(f * lx + q % lx, TILE)
+        extra = spin(ghost_deep[q // lx, pairs + e], GHOST - s, 0)
+        return line_wide(tile, other, jnp.where(sub == GHOST, extra, ghost), ghost)
 
     def load_rows(f, q):
-        main, above, below, j, half, at, turn = pieces(f, q)
-        a, b = above[j], below[j]
-        ghost = spin(jnp.where(sub < GHOST, b, a), GHOST, 0) if half else jnp.where(sub < GHOST, a, b)
-        out = jnp.concatenate([main, ghost], axis=0)
-        return -out if turn else out
+        if q == GZ:
+            return gz_rows[f - DEEP + 1]
+        return line_rows(*pieces(f, q))
 
     row = lax.broadcasted_iota(jnp.int32, (rows, 128), 0)
     lane = lax.broadcasted_iota(jnp.int32, (rows, 128), 1)
     inside = lane % 16
-    ypos = gy * ly + jnp.where(row < ly + GHOST, row, row - rows)
+    ypos = gy * ly + gx * TILE + jnp.where(row < TILE + GHOST, row, row - rows)
     zpos = gz * lz + lane
     zghost = gz * lz + jnp.where(inside < 8, inside - 8, inside + (lz - 8))
 
@@ -629,7 +660,6 @@
         return pltpu.roll(a, 16, 1)
 
     blank = jnp.zeros((rows, 128), f32)
-    zero = jnp.zeros((TILE, 128), f32)
 
     def half_back(ss, yd, zd, yz):
         s = (ss - yd) + y_dn(ss + yd)
@@ -637,7 +667,7 @@
         return s - d, s + d
 
     def damage_sum(q):
-        a = load_wide(6, q)
+        a = load_wide(3, q)
         s = a + z_up(a, gz_wide[3], q)
         return merge(s + y_up(s)), a
 
@@ -657,11 +687,11 @@
     stiff[GZ] = rigidity(taken, plane_up(taken), gvalid)
     stiff[nx - 1] = blank
 
-    def gather_back(ref, planes, emit):
+    def gather_back(ref, emit):
         ghost = ref[GZ]
         below = blank
         taken = pltpu.roll(ghost, 1, 1)
-        for q in range(planes):
+        for q in range(nx):
             a = ref[q]
             s = a + z_dn(a, ghost, q)
             here = s + y_dn(s)
@@ -673,10 +703,8 @@
         emit(GZ, s + plane_dn(s))
 
     def inv_emit(q, total):
-        free = (gz_rows[4] if q == GZ else load_rows(7, q)) > 0.0
+        free = load_rows(7, q) > 0.0
         inverse[q] = jnp.where(free, 1.0 / jnp.where(free, stiff_diag * total, 1.0), 0.0)
-
-    gather_back(stiff, nx, inv_emit)
 
     def forward(u, near_u, keep):
         zs, zd = u + near_u, near_u - u
@@ -687,11 +715,11 @@
     def same(a):
         return a
 
-    def pass_one(load, planes, keep, height, with_ghost):
+    def pass_one(load, keep, height, with_ghost):
         for c in range(3):
             ghost = load(c, GZ)
             taken = pltpu.roll(ghost, 127, 1)
-            for q in range(planes):
+            for q in range(nx):
                 u = load(c, q)
                 out = forward(u, z_up(u, ghost, q), keep)
                 for m in range(4):
@@ -758,26 +786,25 @@
         highs = [FD[m] if FS[m] is None else FS[m] + FD[m] for m in range(12)]
         return lows, highs
 
-    def element_pass(layers, energies, to_end):
+    def element_pass(with_energy):
         def step(chunk, carry):
             r = pl.ds(pl.multiple_of(chunk * TILE, TILE), TILE)
             low = [modes[m, 0, r, :] for m in range(12)]
             held = None
-            for p in range(layers):
+            for p in range(nx - 1):
                 high = [modes[m, p + 1, r, :] for m in range(12)]
                 lows, highs = element(
-                    low, high, stiff[p, r, :], (p, r, slice(None)) if p < energies else None
+                    low, high, stiff[p, r, :], (p, r, slice(None)) if with_energy else None
                 )
                 for m in range(12):
                     modes[m, p, r, :] = lows[m] + held[m] if p else lows[m]
                 held, low = highs, high
-            if to_end:
-                for m in range(12):
-                    modes[m, layers, r, :] = held[m]
+            for m in range(12):
+                modes[m, nx - 1, r, :] = held[m]
             low = [modes[m, GZ, r, :] for m in range(12)]
             lows, highs = element(
                 low, [plane_up(a) for a in low], stiff[GZ, r, :],
-                (GZ, r, slice(None)) if energies else None,
+                (GZ, r, slice(None)) if with_energy else None,
             )
             for m in range(12):
                 modes[m, GZ, r, :] = lows[m] + plane_dn(highs[m])
@@ -785,10 +812,10 @@
 
         lax.fori_loop(0, rows // TILE, step, 0, unroll=True)
 
-    def each_node(planes, emit, carry):
+    def each_node(emit, carry):
         ghosts = [half_back(*(modes[4 * c + m, GZ] for m in range(4))) for c in range(3)]
         taken = [pltpu.roll(g[1], 1, 1) for g in ghosts]
-        for q in range(planes):
+        for q in range(nx):
             got = []
             for c in range(3):
                 near_w, far_w = half_back(*(modes[4 * c + m, q] for m in range(4)))
@@ -798,45 +825,42 @@
         emit(GZ, [ghosts[c][0] + taken[c] for c in range(3)], carry)
         return carry
 
-    def fold(a):
-        total = a[0:TILE]
-        for i in range(TILE, ly, TILE):
-            total = total + a[i : i + TILE]
-        return total
-
     nd, ng = DISP_ITERS, DMG_ITERS
     gram, vector = {}, {}
 
     def load_start(c, q):
         return gz_wide[c] if q == GZ else load_wide(c, q)
 
-    pass_one(load_start, nx, merge, rows, True)
-    element_pass(nx - 1, lx + ng, True)
+    pass_one(load_start, merge, rows, True)
+    element_pass(True)
+    hist[nx - 1] = blank
+    arrive(1)
+    greet(hop_sem)
+    for f in range(DEEP, fields):
+        gz_rows[f - DEEP + 1] = line_rows(*ghost_tiles(f))
+    gather_back(stiff, inv_emit)
 
     def start_emit(q, got, dot):
         inv = inverse[q]
         for c in range(3):
-            force = gz_rows[c] if q == GZ else load_rows(3 + c, q)
-            r = force - got[c]
+            r = load_rows(DEEP + c, q) - got[c]
             v = inv * r
             basis[c, q] = v
-            if q < lx:
-                resid[c, q] = r[0:ly]
-                dot = dot + fold((v * r)[0:ly])
+            if q < nx:
+                resid[c, q] = r[0:TILE]
+                dot = dot + v[0:TILE] * r[0:TILE]
         return dot
 
-    vector[0] = each_node(nx, start_emit, zero)
+    vector[0] = each_node(start_emit, zero)
 
     def hist_emit(q, total):
-        top = gz_rows[4] if q == GZ else load_rows(7, q)
-        react[q] = jnp.maximum(jnp.abs(top), 0.125 * total)
-
-    gather_back(hist, lx + ng, hist_emit)
+        react[q] = jnp.maximum(jnp.abs(load_rows(7, q)), 0.125 * total)
+
+    gather_back(hist, hist_emit)
 
     for k in range(nd - 1):
-        planes = lx + nd - 1 - k
-        pass_one(lambda c, q, k=k: basis[3 * k + c, q], planes + 1, same, rows, True)
-        element_pass(planes, 0, False)
+        pass_one(lambda c, q, k=k: basis[3 * k + c, q], same, rows, True)
+        element_pass(False)
 
         def apply_emit(q, got, carry, k=k):
             carry = list(carry)
@@ -848,29 +872,32 @@
                 if k:
                     v = 2.0 * v - basis[3 * (k - 1) + c, q]
                 basis[3 * (k + 1) + c, q] = v
-                if q < lx:
-                    wi, vi = w[0:ly], v[0:ly]
+                if q < nx:
+                    wi, vi = w[0:TILE], v[0:TILE]
                     if k + 2 < nd:
                         images[3 * k + c, q] = wi
-                    carry[0] = carry[0] + fold(here[0:ly] * wi)
-                    carry[1] = carry[1] + fold(vi * resid[c, q])
-                    carry[2] = carry[2] + fold(vi * wi)
+                    carry[0] = carry[0] + here[0:TILE] * wi
+                    carry[1] = carry[1] + vi * resid[c, q]
+                    carry[2] = carry[2] + vi * wi
                     for j in range(k):
-                        carry[3 + j] = carry[3 + j] + fold(vi * images[3 * j + c, q])
+                        carry[3 + j] = carry[3 + j] + vi * images[3 * j + c, q]
             return tuple(carry)
 
-        got = each_node(planes, apply_emit, (zero,) * (3 + k))
+        got = each_node(apply_emit, (zero,) * (3 + k))
         gram[k, k], vector[k + 1], gram[k + 1, k] = got[:3]
         for j in range(k):
             gram[k + 1, j] = got[3 + j]
 
+    across = pl.ds((1 - gx) * lx, lx)
+    x_basis = xcopy(basis.at[:, across, 0:TILE], basis_part, 2)
+    x_basis.start()
+
     def last_energy():
-        pass_one(lambda c, q: basis[3 * (nd - 1) + c, q], lx + 1, same, ly, False)
-        total, middle = zero, zero
-        for chunk in range(ly // TILE):
-            r = slice(TILE * chunk, TILE * chunk + TILE)
+        pass_one(lambda c, q: basis[3 * (nd - 1) + c, q], same, TILE, False)
+        total = zero
+        for r in (slice(0, TILE),):
             low = [modes[m, 0, r, :] for m in range(12)]
-            for p in range(lx):
+            for p in range(nx - 1):
                 high = [modes[m, p + 1, r, :] for m in range(12)]
                 S = [low[m] + high[m] if m % 4 else None for m in range(12)]
                 D = [high[m] - low[m] for m in range(12)]
@@ -895,12 +922,9 @@
                     + (k_bend * sum_bend + (2.0 * k_cross) * sum_cross)
                     + k_last * sum_last
                 ) * stiff[p, r, :]
-                if p + 1 < lx:
-                    total = total + energy
-                else:
-                    middle = middle + energy
+                total = total + energy
                 low = high
-        return total + 0.5 * middle
+        return total
 
     gram[nd - 1, nd - 1] = last_energy()
 
@@ -921,13 +945,12 @@
         mixed = (n - s) + (2.0 * (cy * slope) + (y_up(slope) + y_dn(slope)))
         return 2.0 * mixed + both, mixed - both
 
-    def laplace_pass(load, planes, emit, carry, with_ghost):
+    def laplace_pass(load, emit, carry, with_ghost):
         ghost = load(GZ)
         after = pltpu.roll(ghost, 127, 1)
         before = pltpu.roll(ghost, 1, 1)
-        reach = planes + 1 if planes < nx else nx
         ahead = []
-        for q in range(reach):
+        for q in range(nx):
             d = load(q)
             ahead.append(lines(d, z_up(d, ghost, q), z_dn(d, ghost, q), cz))
             if with_ghost:
@@ -937,6 +960,7 @@
             if p >= 0:
                 total = ahead[p][0] if p == 0 else 2.0 * ahead[p][0] + ahead[p - 1][1]
                 carry = emit(p, lap_scale * (total + ahead[q][1]), carry)
+        carry = emit(nx - 1, lap_scale * (ahead[nx - 1][0] + ahead[nx - 2][1]), carry)
         if with_ghost:
             inner, outer = lines(ghost, after, before, czg)
             total = cxg * inner + jnp.where(lane >= 16, plane_dn(outer), 0.0)
@@ -948,27 +972,26 @@
         return TOUGHNESS / LENGTH_SCALE + 2.0 * react[q]
 
     def old_damage(q):
-        return gz_rows[3] if q == GZ else load_rows(6, q)
+        return load_rows(3, q)
 
     def dstart(q, lap, dot):
         reaction = reaction_of(q)
         if q == GZ:
             count, mask = cxg * cy * czg, gnode
         else:
-            count, mask = (cy * cz if q == 0 else 2.0 * cy * cz), node
+            count, mask = (cy * cz if q in (0, nx - 1) else 2.0 * cy * cz), node
         inv = mask / (diag_scale * count + reaction)
         dinverse[q] = inv
         r = 2.0 * react[q] - (lap + reaction * old_damage(q))
         v = inv * r
         dbasis[0, q] = v
-        if q < lx:
-            dresid[q] = r[0:ly]
-            dot = dot + fold((v * r)[0:ly])
+        if q < nx:
+            dresid[q] = r[0:TILE]
+            dot = dot + v[0:TILE] * r[0:TILE]
         return dot
 
     dvector, dgram = {}, {}
-    dvector[0] = laplace_pass(old_damage, lx + ng, dstart, zero, True)
-    dimages = {}
+    dvector[0] = laplace_pass(old_damage, dstart, zero, True)
     for k in range(ng):
         more = k + 1 < ng
 
@@ -976,20 +999,20 @@
             carry = list(carry)
             here = dbasis[k, q]
             w = lap + reaction_of(q) * here
-            if q < lx:
-                carry[0] = carry[0] + fold((here * w)[0:ly])
+            if q < nx:
+                carry[0] = carry[0] + here[0:TILE] * w[0:TILE]
             if more:
                 v = dinverse[q] * w - here
                 if k:
                     v = 2.0 * v - dbasis[k - 1, q]
                 dbasis[k + 1, q] = v
-                if q < lx:
-                    carry[1] = carry[1] + fold(v[0:ly] * dresid[q])
-                    carry[2] = carry[2] + fold((v * w)[0:ly])
+                if q < nx:
+                    carry[1] = carry[1] + v[0:TILE] * dresid[q]
+                    carry[2] = carry[2] + v[0:TILE] * w[0:TILE]
             return tuple(carry)
 
         got = laplace_pass(
-            lambda q, k=k: dbasis[k, q], lx + ng - 1 - k, dstep, (zero,) * (3 if more else 1), more
+            lambda q, k=k: dbasis[k, q], dstep, (zero,) * (3 if more else 1), more
         )
         dgram[k, k] = got[0]
         if more:
@@ -1003,27 +1026,45 @@
     for i, piece in enumerate(parts):
         line = jnp.sum(piece, axis=0, keepdims=True)
         packed = jnp.where(at == i, jnp.sum(line, axis=1, keepdims=True), packed)
-    mine = gx * npeer + me
-    sums[mine] = packed
+    slot_mine = gx * npeer + me
+    sums[slot_mine] = packed
     pl.semaphore_wait(hop_sem, number_near)
 
-    def peer_copy(side, o, slot):
-        q = lax.rem(me + o, npeer)
-        k = side * npeer + o
+    def peer(dy, dz):
+        return lax.rem(gy + dy, ngy), lax.rem(gz + dz, ngz)
+
+    def peer_copy(side, dy, dz, slot):
+        k = side * npeer + dy * ngz + dz
         return remote(
-            sums.at[mine], sums.at[slot], asend_sem, arecv_sem, k,
-            (gx if side == 0 else 1 - gx, q // ngz, lax.rem(q, ngz)),
+            sums.at[slot_mine], sums.at[slot], asend_sem.at[k], arecv_sem.at[k],
+            (gx if side == 0 else 1 - gx, *peer(dy, dz)),
         )
 
-    peers = [(side, o) for o in range(npeer) for side in (0, 1) if side or o]
-    sends = [peer_copy(side, o, mine) for side, o in peers]
+    offsets = sorted(
+        [(dy, dz) for dy in range(ngy) for dz in range(ngz)],
+        key=lambda o: -(2 * (o[1] % 2) + (o[1] > 0) + o[0] % 2 + (o[0] > 0)),
+    )
+    peers = [(side, dy, dz) for dy, dz in offsets for side in (0, 1) if side or dy or dz]
+    sends = [peer_copy(side, dy, dz, slot_mine) for side, dy, dz in peers]
     for s in sends:
         s.start()
-    for q in range(lx):
-        out_history[place(q)] = react[q, 0:ly]
-    for side, o in peers:
+    x_damage = xcopy(dbasis.at[:, across, 0:TILE], dbasis_part, 3)
+    x_damage.start()
+    x_react = xcopy(react.at[across, 0:TILE], react_part, 4)
+    x_react.start()
+    x_parts = [x_basis, x_damage, x_react]
+    for passed in x_parts:
+        passed.wait_recv()
+
+    def both_tiles(near_tile, far_tile):
+        return jnp.concatenate(order(near_tile, far_tile), axis=0)
+
+    for p in range(lx):
+        out_history[p] = both_tiles(react[gx * lx + p, 0:TILE], react_part[p])
+    for side, dy, dz in peers:
         from_x = gx if side == 0 else 1 - gx
-        peer_copy(side, o, from_x * npeer + lax.rem(me + npeer - o, npeer)).wait_recv()
+        from_y, from_z = peer(ngy - dy, ngz - dz)
+        peer_copy(side, dy, dz, from_x * npeer + from_y * ngz + from_z).wait_recv()
     layer = [sums[i] for i in range(2 * npeer)]
     while len(layer) > 1:
         layer = [a + b for a, b in zip(layer[::2], layer[1::2])] + layer[len(layer) & ~1 :]
@@ -1059,22 +1100,28 @@
     cut = nd * (nd + 1) // 2
     weights = solve(scalars[:nd], triangle(rest[:cut], nd))
     dweights = solve(scalars[nd : nd + ng], triangle(rest[cut:], ng))
-    for q in range(lx):
-        p = place(q)
+    for p in range(lx):
+        at_x = gx * lx + p
         for c in range(3):
-            x = own[c, q]
+            near_x = far_x = zero
             for k in range(nd):
-                x = x + weights[k] * basis[3 * k + c, q, 0:ly]
-            out_disp[c, p] = sign * x if c == 0 else x
-        d = own[6, q]
+                near_x = near_x + weights[k] * basis[3 * k + c, at_x, 0:TILE]
+                far_x = far_x + weights[k] * basis_part[3 * k + c, p]
+            lower, upper = order(near_x, far_x)
+            out_disp[c, p, 0:TILE] = full_deep[c, 0, at_x] + lower
+            out_disp[c, p, TILE:ly] = full_deep[c, 1, at_x] + upper
+        near_d = far_d = zero
         for k in range(ng):
-            d = d + dweights[k] * dbasis[k, q, 0:ly]
-        out_damage[p] = d
-
-    for way in order:
-        pl.when(there(*way))(halos[way].wait_send)
-    for exchange in (x_own, x_z, x_up, x_down):
-        exchange.wait_send()
+            near_d = near_d + dweights[k] * dbasis[k, at_x, 0:TILE]
+            far_d = far_d + dweights[k] * dbasis_part[k, p]
+        lower, upper = order(near_d, far_d)
+        out_damage[p, 0:TILE] = full_deep[3, 0, at_x] + lower
+        out_damage[p, TILE:ly] = full_deep[3, 1, at_x] + upper
+
+    for guard, copy in halos[0] + halos[1]:
+        pl.when(guard)(copy.wait_send)
+    for passed in x_own + x_parts:
+        passed.wait_send()
     for s in sends:
         s.wait_send()
 
@@ -1093,8 +1140,8 @@
 
 def body_fused(sizes, *arrays):
     ngy, ngz, lx, ly, lz = sizes
-    nx, rows, wide, fields = 2 * lx, ly + TILE, ly + 2 * TILE, 8
-    packs, pairs, extras = fields * lx // 16, fields * lx // 2, len(DEEP) * lx // TILE
+    nx, rows, wide, fields = 2 * lx, 2 * TILE, 3 * TILE, 8
+    packs, pairs, extras = fields * lx // 16, DEEP * lx // 2, DEEP * lx // TILE
     npeer = ngy * ngz
     f32 = jnp.float32
     planes = (nx + 1, rows, lz)
@@ -1121,40 +1168,44 @@
             room(lx, ly, lz),
             pltpu.VMEM((lx, ly, lz), jnp.int32),
             pltpu.VMEM((lx, ly, lz), jnp.int32),
-            room(fields, lx, ly, lz),
-            room(fields, lx, ly, lz),
+            room(DEEP, 2, nx, TILE, lz),
+            room(DEEP, 2, nx, TILE, lz),
             room(pairs + extras, TILE, 128),
             room(pairs, TILE, 128),
-            room(pairs + extras, TILE, 128),
             room(pairs, TILE, 128),
-            room(pairs + extras, TILE, 128),
             room(pairs, TILE, 128),
-            room(2, packs, ly, 128),
-            room(2, packs, wide, 128),
-            room(2, packs, wide, 128),
+            room(2, pairs + extras, TILE, 128),
+            room(2, pairs, TILE, 128),
+            room(2, 2, TILE, 128),
+            room(2, 2, TILE, 128),
+            room(2, 2, 3, TILE, 128),
+            room(2, 2, 3, TILE, 128),
             room(4, wide, 128),
             room(5, rows, 128),
             room(12, *planes),
             room(3 * DISP_ITERS, *planes),
-            room(3 * (DISP_ITERS - 2), lx, ly, lz),
-            room(3, lx, ly, lz),
+            room(3 * (DISP_ITERS - 2), nx, TILE, lz),
+            room(3, nx, TILE, lz),
             room(*planes),
             room(*planes),
             room(*planes),
             room(*planes),
             room(*planes),
             room(DMG_ITERS, *planes),
-            room(lx, ly, lz),
+            room(nx, TILE, lz),
+            room(3 * DISP_ITERS, lx, TILE, lz),
+            room(DMG_ITERS, lx, TILE, lz),
+            room(lx, TILE, lz),
             room(2 * npeer, 1, 128),
             dma((6,)),
-            dma((2,)),
-            dma((2,)),
-            dma((2,)),
-            dma((2,)),
             dma((4,)),
             dma((4,)),
-            dma((4,)),
-            dma((4,)),
+            dma((8,)),
+            dma((8,)),
+            dma((8,)),
+            dma((8,)),
+            dma((5,)),
+            dma((5,)),
             dma((2 * npeer,)),
             dma((2 * npeer,)),
             pltpu.SemaphoreType.REGULAR,
@@ -1183,7 +1234,7 @@
         lx, ly, lz = arrays[2].shape
         fits = shape["gx"] == 2 and shape["gy"] * shape["gz"] > 1
         fits = fits and max(shape["gy"], shape["gz"]) <= 4
-        fits = fits and lx == 4 and ly % 8 == 0 and lz == 128
+        fits = fits and lx == 4 and ly == 2 * TILE and lz == 128
         if fits:
             return body_fused((shape["gy"], shape["gz"], lx, ly, lz), *arrays)
         return body_any_mesh(*arrays)

time: 23.6 us -> 21.8 us (0.924)
  Pallas kernels: 22.8 us -> 21 us
    pallas_call x1, Pallas kernels: 22.1 us -> 20.3 us  [body_fused(): pl.pallas_call(functools.partial(kernel, sizes), out_shape=(pltpu.VMEM((3...]
where the time goes in v3:
time: 21.8 us; the launch traced here: 21.6 us
  Pallas kernels  21 us (96%)
  between operations  0.64 us (3%)
    pallas_call x1, Pallas kernels, body_fused(): pl.pallas_call(functools.partial(kernel, sizes), out_shape=(pltpu.VMEM((3...  20.3 us
    pallas_call x1, Pallas kernels, body_fused(): pl.pallas_call(hand_on, out_shape=tuple((jax.ShapeDtypeStruct(r.shape, f3...  0.69 us

profile of v3, /device:TPU:0, one launch (start us, length us, event | category | flops | bytes accessed | tf_op | source)
XLA Modules:
  0.0 21.6 jit_solution(6554605957469755546)
XLA Ops:
  0.6 20.3 %shard_map.85 = (f32[3,4,16,128]{3,2,1,0:T(8,128)S(1)}, f32[4,16,128]{2,1,0:T(8,128)S(1)}, f32[4,16,128]{2,1,0:T(8,128)S(1)}) custom-call(f32[3,4,16,128]{3,2,1,0:T(8,128)} %disp_in.1, f32[3,4,16,128]{3,2,1,0:T(8,128)} %force_in.1, f32[4,16,128]{2,1,0:T(8,128)} %damage_in.1, f32[4,16,128]{2,1,0:T(8,128)} %history_in.1, s32[4,16,128]{2,1,0:T(8,128)} %labels_in.1, ...), custom_call_target="tpu_custom_call" | custom-call | tf_op jit(solution)/shard_map/pallas_call | solution.py:1155
  20.9 0.7 %shard_map.86 = (f32[3,4,16,128]{3,2,1,0:T(8,128)}, f32[4,16,128]{2,1,0:T(8,128)}, f32[4,16,128]{2,1,0:T(8,128)}) custom-call(f32[3,4,16,128]{3,2,1,0:T(8,128)S(1)} %get-tuple-element.6.refs_0_, f32[4,16,128]{2,1,0:T(8,128)S(1)} %get-tuple-element.7.refs_1_, f32[4,16,128]{2,1,0:T(8,128)S(1)} %get-tuple-element.8.refs_2_), custom_call_target="tpu_custom_call" | custom-call | tf_op jit(solution)/shard_map/pallas_call | solution.py:1217

commit v4 on v3

--- a/solution.py
+++ b/solution.py
@@ -504,7 +504,7 @@
         side = 0 if dz < 0 else 1
         return remote(
             zsend[pack].at[side], zbuf[pack].at[source, side, 0:2],
-            zsend_sem.at[4 * core + 2 * side + pack], zrecv_sem.at[4 * source + 2 * side + pack],
+            zsend_sem.at[side], zrecv_sem.at[2 * side + pack],
             device(core, 0, dz),
         )
 
@@ -512,8 +512,8 @@
         side = 0 if dz < 0 else 1
         return remote(
             zsend[pack].at[side, int(dy > 0)], zbuf[pack].at[source, side, 2],
-            csend_sem.at[4 * (dy > 0) + 2 * side + pack],
-            crecv_sem.at[4 * source + 2 * side + pack],
+            csend_sem.at[2 * (dy > 0) + side],
+            crecv_sem.at[2 * side + pack],
             device(int(dy < 0), dy, dz),
         )
 
@@ -525,7 +525,7 @@
         else:
             src, dst = up_deep, ghost_deep.at[source, 0:pairs]
         return remote(
-            src, dst, ysend_sem.at[2 * flat + (dy > 0)], yrecv_sem.at[2 * flat + source],
+            src, dst, ysend_sem.at[2 * flat + (dy > 0)], yrecv_sem.at[flat],
             device(int(dy < 0), dy, 0),
         )
 
@@ -545,19 +545,26 @@
         for guard, copy in halos[flat]:
             pl.when(guard)(copy.start)
 
+    def drain(ref, send, recv):
+        return remote(ref, ref, send, recv, partner)
+
     def arrive(flat):
-        for dz in (-1, 1):
-            for source in range(2):
-                pl.when(there(0, -dz))(zcopy(source, dz, flat, 0).wait_recv)
+        for side, dz in ((0, -1), (1, 1)):
+            faces = zbuf[flat].at[:, side, 0:2]
+            pl.when(there(0, -dz))(
+                drain(faces, zsend_sem.at[side], zrecv_sem.at[2 * side + flat]).wait_recv
+            )
         x_own[flat].wait_recv()
-        for dz in (-1, 1):
-            for source in range(2):
-                pl.when(there(outward, -dz))(corner(source, 1, dz, flat).wait_recv)
+        for side, dz in ((0, -1), (1, 1)):
+            edges = zbuf[flat].at[:, side, 2]
+            pl.when(there(outward, -dz))(
+                drain(edges, csend_sem.at[side], crecv_sem.at[2 * side + flat]).wait_recv
+            )
+        rows_in = [ghost_flat] * 2 if flat else [ghost_deep.at[:, 0:pairs], ghost_deep]
         for core in range(2):
-            for source in range(2):
-                pl.when((gx == core) & there(outward, 0))(
-                    ycopy(source, -1 if core else 1, flat).wait_recv
-                )
+            pl.when((gx == core) & there(outward, 0))(
+                drain(rows_in[core], ysend_sem.at[flat], yrecv_sem.at[flat]).wait_recv
+            )
 
     arrive(0)
 
@@ -1034,9 +1041,8 @@
         return lax.rem(gy + dy, ngy), lax.rem(gz + dz, ngz)
 
     def peer_copy(side, dy, dz, slot):
-        k = side * npeer + dy * ngz + dz
         return remote(
-            sums.at[slot_mine], sums.at[slot], asend_sem.at[k], arecv_sem.at[k],
+            sums.at[slot_mine], sums.at[slot], asend_sem.at[0], arecv_sem.at[0],
             (gx if side == 0 else 1 - gx, *peer(dy, dz)),
         )
 
@@ -1061,10 +1067,8 @@
 
     for p in range(lx):
         out_history[p] = both_tiles(react[gx * lx + p, 0:TILE], react_part[p])
-    for side, dy, dz in peers:
-        from_x = gx if side == 0 else 1 - gx
-        from_y, from_z = peer(ngy - dy, ngz - dz)
-        peer_copy(side, dy, dz, from_x * npeer + from_y * ngz + from_z).wait_recv()
+    everyone = drain(sums.at[0 : 2 * npeer - 1], asend_sem.at[0], arecv_sem.at[0])
+    everyone.wait_recv()
     layer = [sums[i] for i in range(2 * npeer)]
     while len(layer) > 1:
         layer = [a + b for a, b in zip(layer[::2], layer[1::2])] + layer[len(layer) & ~1 :]
@@ -1118,12 +1122,20 @@
         out_damage[p, 0:TILE] = full_deep[3, 0, at_x] + lower
         out_damage[p, TILE:ly] = full_deep[3, 1, at_x] + upper
 
-    for guard, copy in halos[0] + halos[1]:
-        pl.when(guard)(copy.wait_send)
+    for side, dz in ((0, -1), (1, 1)):
+        pl.when(there(0, dz))(
+            drain(full_deep.at[0, 0], zsend_sem.at[side], zrecv_sem.at[0]).wait_send
+        )
+        for dy in (-1, 1):
+            pl.when(there(dy, dz))(
+                drain(zsend_deep.at[side], csend_sem.at[2 * (dy > 0) + side], crecv_sem.at[0]).wait_send
+            )
+    for flat in range(2):
+        for dy in (-1, 1):
+            pl.when(there(dy, 0))(ycopy(0, dy, flat).wait_send)
     for passed in x_own + x_parts:
         passed.wait_send()
-    for s in sends:
-        s.wait_send()
+    everyone.wait_send()
 
 
 def hand_on(*refs):
@@ -1199,15 +1211,15 @@
             room(2 * npeer, 1, 128),
             dma((6,)),
             dma((4,)),
+            dma((2,)),
+            dma((2,)),
             dma((4,)),
-            dma((8,)),
-            dma((8,)),
-            dma((8,)),
-            dma((8,)),
+            dma((4,)),
+            dma((4,)),
             dma((5,)),
             dma((5,)),
-            dma((2 * npeer,)),
-            dma((2 * npeer,)),
+            dma((1,)),
+            dma((1,)),
             pltpu.SemaphoreType.REGULAR,
         ],
         compiler_params=pltpu.CompilerParams(

time: 21.8 us -> 20.9 us (0.959)
  Pallas kernels: 21 us -> 20.1 us
    pallas_call x1, Pallas kernels: 20.3 us -> 19.5 us  [body_fused(): pl.pallas_call(functools.partial(kernel, sizes), out_shape=(pltpu.VMEM((3...]
where the time goes in v4:
time: 20.9 us; the launch traced here: 20.8 us
  Pallas kernels  20.1 us (96%)
  between operations  0.64 us (3%)
    pallas_call x1, Pallas kernels, body_fused(): pl.pallas_call(functools.partial(kernel, sizes), out_shape=(pltpu.VMEM((3...  19.5 us
    pallas_call x1, Pallas kernels, body_fused(): pl.pallas_call(hand_on, out_shape=tuple((jax.ShapeDtypeStruct(r.shape, f3...  0.69 us

profile of v4, /device:TPU:0, one launch (start us, length us, event | category | flops | bytes accessed | tf_op | source)
XLA Modules:
  0.0 20.8 jit_solution(88669322845533523)
XLA Ops:
  0.6 19.5 %shard_map.85 = (f32[3,4,16,128]{3,2,1,0:T(8,128)S(1)}, f32[4,16,128]{2,1,0:T(8,128)S(1)}, f32[4,16,128]{2,1,0:T(8,128)S(1)}) custom-call(f32[3,4,16,128]{3,2,1,0:T(8,128)} %disp_in.1, f32[3,4,16,128]{3,2,1,0:T(8,128)} %force_in.1, f32[4,16,128]{2,1,0:T(8,128)} %damage_in.1, f32[4,16,128]{2,1,0:T(8,128)} %history_in.1, s32[4,16,128]{2,1,0:T(8,128)} %labels_in.1, ...), custom_call_target="tpu_custom_call" | custom-call | tf_op jit(solution)/shard_map/pallas_call | solution.py:1167
  20.1 0.7 %shard_map.86 = (f32[3,4,16,128]{3,2,1,0:T(8,128)}, f32[4,16,128]{2,1,0:T(8,128)}, f32[4,16,128]{2,1,0:T(8,128)}) custom-call(f32[3,4,16,128]{3,2,1,0:T(8,128)S(1)} %get-tuple-element.6.refs_0_, f32[4,16,128]{2,1,0:T(8,128)S(1)} %get-tuple-element.7.refs_1_, f32[4,16,128]{2,1,0:T(8,128)S(1)} %get-tuple-element.8.refs_2_), custom_call_target="tpu_custom_call" | custom-call | tf_op jit(solution)/shard_map/pallas_call | solution.py:1229

commit v5 on v4

--- a/solution.py
+++ b/solution.py
@@ -399,24 +399,21 @@
                         semaphore, inc=1, device_id=device(core, dy, dz), device_id_type=MESH
                     )
 
-    greet(barrier)
-    pl.semaphore_signal(barrier, inc=1, device_id=partner, device_id_type=MESH)
-
     loads = [
         pltpu.make_async_copy(source, target, in_sem.at[i])
-        for i, (source, target) in enumerate(
-            [
-                (flags_in, flags_ref),
-                (disp_in, disp_ref),
-                (force_in, force_ref),
-                (damage_in, damage_ref),
-                (history_in, history_ref),
-                (labels_in, labels_ref),
-            ]
+        for source, target, i in (
+            (flags_in, flags_ref, 1),
+            (disp_in, disp_ref, 0),
+            (damage_in, damage_ref, 1),
+            (force_in, force_ref, 0),
+            (history_in, history_ref, 1),
+            (labels_in, labels_ref, 1),
         )
     ]
     for load in loads:
         load.start()
+    greet(barrier)
+    pl.semaphore_signal(barrier, inc=1, device_id=partner, device_id_type=MESH)
 
     zero = jnp.zeros((TILE, 128), f32)
     for dz, side in ((1, 0), (-1, 1)):
@@ -438,8 +435,8 @@
         ghost_deep[...] = jnp.zeros(ghost_deep.shape, f32)
         ghost_flat[...] = jnp.zeros(ghost_flat.shape, f32)
 
-    for load in loads:
-        load.wait()
+    for i, room in enumerate((basis_part, full_deep.at[0:2])):
+        pltpu.make_async_copy(room, room, in_sem.at[i]).wait()
 
     values = []
     for p in range(lx):
@@ -475,19 +472,19 @@
         for half in range(2):
             zsend[j][0, half] = low[TILE * half : TILE * half + TILE]
             zsend[j][1, half] = high[TILE * half : TILE * half + TILE]
-    for first, down, up in ((0, down_deep, up_deep), (DEEP, down_flat, up_flat)):
+    for first, skip, down, up in ((0, extras, down_deep, up_deep), (DEEP, 0, down_flat, up_flat)):
         for j in range(pairs):
             fa, qa = divmod(2 * j, lx)
             fb, qb = divmod(2 * j + 1, lx)
             a, b = values[qa][first + fa], values[qb][first + fb]
-            down[j] = jnp.where(sub < GHOST, a[0:TILE], spin(b[0:TILE], GHOST, 0))
-            up[j] = jnp.where(sub < GHOST, spin(b[ly - TILE : ly], GHOST, 0), a[ly - TILE : ly])
+            down[skip + j] = jnp.where(sub < GHOST, a[0:TILE], spin(b[0:TILE], GHOST, 0))
+            up[skip + j] = jnp.where(sub < GHOST, spin(b[ly - TILE : ly], GHOST, 0), a[ly - TILE : ly])
     for e in range(extras):
         tile = jnp.zeros((TILE, 128), f32)
         for s in range(TILE):
             f, q = divmod(TILE * e + s, lx)
             tile = jnp.where(sub == s, spin(values[q][f][0:TILE], s - GHOST, 0), tile)
-        down_deep[pairs + e] = tile
+        down_deep[e] = tile
 
     pl.semaphore_wait(barrier, number_near + 1)
 
@@ -517,15 +514,18 @@
             device(int(dy < 0), dy, dz),
         )
 
-    def ycopy(source, dy, flat):
-        if flat:
+    last = extras + 3 * lx // 2
+    tiles_of = {0: slice(extras, last), 2: slice(last, extras + pairs)}
+
+    def ycopy(source, dy, kind):
+        if kind == 1:
             src, dst = (down_flat if dy < 0 else up_flat), ghost_flat.at[source]
-        elif dy < 0:
-            src, dst = down_deep, ghost_deep.at[source]
         else:
-            src, dst = up_deep, ghost_deep.at[source, 0:pairs]
+            tiles = slice(0, last) if dy < 0 and kind == 0 else tiles_of[kind]
+            src = (down_deep if dy < 0 else up_deep).at[tiles]
+            dst = ghost_deep.at[source, tiles]
         return remote(
-            src, dst, ysend_sem.at[2 * flat + (dy > 0)], yrecv_sem.at[flat],
+            src, dst, ysend_sem.at[2 * kind + (dy > 0)], yrecv_sem.at[kind],
             device(int(dy < 0), dy, 0),
         )
 
@@ -536,8 +536,10 @@
     halos = [[], []]
     for flat in (0, 1):
         for source in (0, 1):
-            ways = [((dy, dz), corner(source, dy, dz, flat)) for dy in (-1, 1) for dz in (-1, 1)]
-            ways += [((dy, 0), ycopy(source, dy, flat)) for dy in (-1, 1)]
+            ways = []
+            for dy in (1, -1):
+                ways += [((dy, dz), corner(source, dy, dz, flat)) for dz in (-1, 1)]
+                ways += [((dy, 0), ycopy(source, dy, kind)) for kind in ((1,) if flat else (0, 2))]
             ways += [((0, dz), zcopy(source, dz, flat, core)) for dz in (-1, 1) for core in (0, 1)]
             halos[flat] += [((gx == source) & there(*way), copy) for way, copy in ways]
     for flat in (0, 1):
@@ -560,7 +562,7 @@
             pl.when(there(outward, -dz))(
                 drain(edges, csend_sem.at[side], crecv_sem.at[2 * side + flat]).wait_recv
             )
-        rows_in = [ghost_flat] * 2 if flat else [ghost_deep.at[:, 0:pairs], ghost_deep]
+        rows_in = [ghost_flat] * 2 if flat else [ghost_deep.at[:, tiles_of[0]], ghost_deep.at[:, 0:last]]
         for core in range(2):
             pl.when((gx == core) & there(outward, 0))(
                 drain(rows_in[core], ysend_sem.at[flat], yrecv_sem.at[flat]).wait_recv
@@ -610,14 +612,14 @@
     def pieces(f, q):
         source, p = divmod(q, lx)
         j, half = divmod(f % DEEP * lx + p, 2)
-        ghost = ghost_deep[source, j] if f < DEEP else ghost_flat[source, j]
+        ghost = ghost_deep[source, extras + j] if f < DEEP else ghost_flat[source, j]
         ref = full[f // DEEP]
         return *order(ref[f % DEEP, 0, q], ref[f % DEEP, 1, q]), spin(ghost, GHOST * half, 0)
 
     def load_wide(f, q):
         tile, other, ghost = pieces(f, q)
         e, s = divmod(f * lx + q % lx, TILE)
-        extra = spin(ghost_deep[q // lx, pairs + e], GHOST - s, 0)
+        extra = spin(ghost_deep[q // lx, e], GHOST - s, 0)
         return line_wide(tile, other, jnp.where(sub == GHOST, extra, ghost), ghost)
 
     def load_rows(f, q):
@@ -682,17 +684,6 @@
         rest = 1.0 - (low + high) * 0.125
         return (rest * rest + RESIDUAL_STIFFNESS) * mask
 
-    low, a = damage_sum(0)
-    taken = z_up_take(pltpu.roll(gz_wide[3], 127, 1), a, 0)
-    for q in range(nx - 1):
-        high, a = damage_sum(q + 1)
-        stiff[q] = rigidity(low, high, valid)
-        taken = z_up_take(taken, a, q + 1)
-        low = high
-    taken = gz_wide[3] + taken
-    taken = merge(taken + y_up(taken))
-    stiff[GZ] = rigidity(taken, plane_up(taken), gvalid)
-    stiff[nx - 1] = blank
 
     def gather_back(ref, emit):
         ghost = ref[GZ]
@@ -839,10 +830,24 @@
         return gz_wide[c] if q == GZ else load_wide(c, q)
 
     pass_one(load_start, merge, rows, True)
+    pl.when(there(outward, 0))(
+        drain(ghost_deep.at[:, tiles_of[2]], ysend_sem.at[0], yrecv_sem.at[2]).wait_recv
+    )
+    low, a = damage_sum(0)
+    taken = z_up_take(pltpu.roll(gz_wide[3], 127, 1), a, 0)
+    for q in range(nx - 1):
+        high, a = damage_sum(q + 1)
+        stiff[q] = rigidity(low, high, valid)
+        taken = z_up_take(taken, a, q + 1)
+        low = high
+    taken = gz_wide[3] + taken
+    taken = merge(taken + y_up(taken))
+    stiff[GZ] = rigidity(taken, plane_up(taken), gvalid)
+    stiff[nx - 1] = blank
     element_pass(True)
     hist[nx - 1] = blank
+    greet(hop_sem)
     arrive(1)
-    greet(hop_sem)
     for f in range(DEEP, fields):
         gz_rows[f - DEEP + 1] = line_rows(*ghost_tiles(f))
     gather_back(stiff, inv_emit)
@@ -1130,9 +1135,9 @@
             pl.when(there(dy, dz))(
                 drain(zsend_deep.at[side], csend_sem.at[2 * (dy > 0) + side], crecv_sem.at[0]).wait_send
             )
-    for flat in range(2):
+    for kind in range(3):
         for dy in (-1, 1):
-            pl.when(there(dy, 0))(ycopy(0, dy, flat).wait_send)
+            pl.when(there(dy, 0))(ycopy(0, dy, kind).wait_send)
     for passed in x_own + x_parts:
         passed.wait_send()
     everyone.wait_send()
@@ -1183,7 +1188,7 @@
             room(DEEP, 2, nx, TILE, lz),
             room(DEEP, 2, nx, TILE, lz),
             room(pairs + extras, TILE, 128),
-            room(pairs, TILE, 128),
+            room(pairs + extras, TILE, 128),
             room(pairs, TILE, 128),
             room(pairs, TILE, 128),
             room(2, pairs + extras, TILE, 128),
@@ -1209,9 +1214,9 @@
             room(DMG_ITERS, lx, TILE, lz),
             room(lx, TILE, lz),
             room(2 * npeer, 1, 128),
+            dma((2,)),
             dma((6,)),
-            dma((4,)),
-            dma((2,)),
+            dma((3,)),
             dma((2,)),
             dma((4,)),
             dma((4,)),

time: 20.9 us -> 20.4 us (0.976)
  Pallas kernels: 20.1 us -> 19.6 us
    pallas_call x1, Pallas kernels: 19.5 us -> 19 us  [body_fused(): pl.pallas_call(functools.partial(kernel, sizes), out_shape=(pltpu.VMEM((3...]
where the time goes in v5:
time: 20.4 us; the launch traced here: 20.3 us
  Pallas kernels  19.6 us (96%)
  between operations  0.64 us (3%)
    pallas_call x1, Pallas kernels, body_fused(): pl.pallas_call(functools.partial(kernel, sizes), out_shape=(pltpu.VMEM((3...  19 us
    pallas_call x1, Pallas kernels, body_fused(): pl.pallas_call(hand_on, out_shape=tuple((jax.ShapeDtypeStruct(r.shape, f3...  0.69 us

profile of v5, /device:TPU:0, one launch (start us, length us, event | category | flops | bytes accessed | tf_op | source)
XLA Modules:
  0.0 20.3 jit_solution(4007504518505319636)
XLA Ops:
  0.6 19.0 %shard_map.85 = (f32[3,4,16,128]{3,2,1,0:T(8,128)S(1)}, f32[4,16,128]{2,1,0:T(8,128)S(1)}, f32[4,16,128]{2,1,0:T(8,128)S(1)}) custom-call(f32[3,4,16,128]{3,2,1,0:T(8,128)} %disp_in.1, f32[3,4,16,128]{3,2,1,0:T(8,128)} %force_in.1, f32[4,16,128]{2,1,0:T(8,128)} %damage_in.1, f32[4,16,128]{2,1,0:T(8,128)} %history_in.1, s32[4,16,128]{2,1,0:T(8,128)} %labels_in.1, ...), custom_call_target="tpu_custom_call" | custom-call | tf_op jit(solution)/shard_map/pallas_call | solution.py:1172
  19.6 0.7 %shard_map.86 = (f32[3,4,16,128]{3,2,1,0:T(8,128)}, f32[4,16,128]{2,1,0:T(8,128)}, f32[4,16,128]{2,1,0:T(8,128)}) custom-call(f32[3,4,16,128]{3,2,1,0:T(8,128)S(1)} %get-tuple-element.6.refs_0_, f32[4,16,128]{2,1,0:T(8,128)S(1)} %get-tuple-element.7.refs_1_, f32[4,16,128]{2,1,0:T(8,128)S(1)} %get-tuple-element.8.refs_2_), custom_call_target="tpu_custom_call" | custom-call | tf_op jit(solution)/shard_map/pallas_call | solution.py:1234

commit v6 on v5

--- a/solution.py
+++ b/solution.py
@@ -533,19 +533,21 @@
     x_own = [
         xcopy(full[flat].at[:, :, own], full[flat].at[:, :, own], flat) for flat in range(2)
     ]
-    halos = [[], []]
-    for flat in (0, 1):
-        for source in (0, 1):
-            ways = []
-            for dy in (1, -1):
-                ways += [((dy, dz), corner(source, dy, dz, flat)) for dz in (-1, 1)]
+    halos = []
+    for dy in (1, -1):
+        for flat in (0, 1):
+            for source in (0, 1):
+                ways = [((dy, dz), corner(source, dy, dz, flat)) for dz in (-1, 1)]
                 ways += [((dy, 0), ycopy(source, dy, kind)) for kind in ((1,) if flat else (0, 2))]
-            ways += [((0, dz), zcopy(source, dz, flat, core)) for dz in (-1, 1) for core in (0, 1)]
-            halos[flat] += [((gx == source) & there(*way), copy) for way, copy in ways]
-    for flat in (0, 1):
-        x_own[flat].start()
-        for guard, copy in halos[flat]:
-            pl.when(guard)(copy.start)
+                if dy > 0:
+                    ways += [
+                        ((0, dz), zcopy(source, dz, flat, core)) for dz in (-1, 1) for core in (0, 1)
+                    ]
+                halos += [((gx == source) & there(*way), copy) for way, copy in ways]
+    for exchange in x_own:
+        exchange.start()
+    for guard, copy in halos:
+        pl.when(guard)(copy.start)
 
     def drain(ref, send, recv):
         return remote(ref, ref, send, recv, partner)
@@ -823,6 +825,52 @@
         emit(GZ, [ghosts[c][0] + taken[c] for c in range(3)], carry)
         return carry
 
+    cy = yvalid + element_at(ypos - 1, ngy * ly)
+    cz = element_at(zpos, ngz * lz) + element_at(zpos - 1, ngz * lz)
+    czg = element_at(zghost, ngz * lz) + element_at(zghost - 1, ngz * lz)
+    cxg = jnp.where((lane < 16) | (lane >= 16 * (nx - 1)), 1.0, 2.0)
+    node = jnp.where(cy * cz > 0.0, 1.0, 0.0)
+    gnode = jnp.where(cy * czg > 0.0, 1.0, 0.0)
+    diag_scale = laplace_diag * TOUGHNESS * LENGTH_SCALE
+    lap_scale = TOUGHNESS * LENGTH_SCALE / 36.0
+
+    def lines(d, after, before, count_z):
+        s, n = after + before, count_z * d
+        mass, slope = 2.0 * n + s, n - s
+        s, n = y_up(mass) + y_dn(mass), cy * mass
+        both = 2.0 * n + s
+        mixed = (n - s) + (2.0 * (cy * slope) + (y_up(slope) + y_dn(slope)))
+        return 2.0 * mixed + both, mixed - both
+
+    def laplace_pass(load, emit, carry, with_ghost):
+        ghost = load(GZ)
+        after = pltpu.roll(ghost, 127, 1)
+        before = pltpu.roll(ghost, 1, 1)
+        ahead = []
+        for q in range(nx):
+            d = load(q)
+            ahead.append(lines(d, z_up(d, ghost, q), z_dn(d, ghost, q), cz))
+            if with_ghost:
+                after = z_up_take(after, d, q)
+                before = z_dn_take(before, d, q)
+            p = q - 1
+            if p >= 0:
+                total = ahead[p][0] if p == 0 else 2.0 * ahead[p][0] + ahead[p - 1][1]
+                carry = emit(p, lap_scale * (total + ahead[q][1]), carry)
+        carry = emit(nx - 1, lap_scale * (ahead[nx - 1][0] + ahead[nx - 2][1]), carry)
+        if with_ghost:
+            inner, outer = lines(ghost, after, before, czg)
+            total = cxg * inner + jnp.where(lane >= 16, plane_dn(outer), 0.0)
+            total = total + jnp.where(lane < 16 * (nx - 1), plane_up(outer), 0.0)
+            emit(GZ, lap_scale * total, carry)
+        return carry
+
+    def reaction_of(q):
+        return TOUGHNESS / LENGTH_SCALE + 2.0 * react[q]
+
+    def old_damage(q):
+        return load_rows(3, q)
+
     nd, ng = DISP_ITERS, DMG_ITERS
     gram, vector = {}, {}
 
@@ -847,6 +895,12 @@
     element_pass(True)
     hist[nx - 1] = blank
     greet(hop_sem)
+
+    def keep_lap(q, lap, carry):
+        dbasis[0, q] = lap
+        return carry
+
+    laplace_pass(old_damage, keep_lap, zero, True)
     arrive(1)
     for f in range(DEEP, fields):
         gz_rows[f - DEEP + 1] = line_rows(*ghost_tiles(f))
@@ -940,52 +994,6 @@
 
     gram[nd - 1, nd - 1] = last_energy()
 
-    cy = yvalid + element_at(ypos - 1, ngy * ly)
-    cz = element_at(zpos, ngz * lz) + element_at(zpos - 1, ngz * lz)
-    czg = element_at(zghost, ngz * lz) + element_at(zghost - 1, ngz * lz)
-    cxg = jnp.where((lane < 16) | (lane >= 16 * (nx - 1)), 1.0, 2.0)
-    node = jnp.where(cy * cz > 0.0, 1.0, 0.0)
-    gnode = jnp.where(cy * czg > 0.0, 1.0, 0.0)
-    diag_scale = laplace_diag * TOUGHNESS * LENGTH_SCALE
-    lap_scale = TOUGHNESS * LENGTH_SCALE / 36.0
-
-    def lines(d, after, before, count_z):
-        s, n = after + before, count_z * d
-        mass, slope = 2.0 * n + s, n - s
-        s, n = y_up(mass) + y_dn(mass), cy * mass
-        both = 2.0 * n + s
-        mixed = (n - s) + (2.0 * (cy * slope) + (y_up(slope) + y_dn(slope)))
-        return 2.0 * mixed + both, mixed - both
-
-    def laplace_pass(load, emit, carry, with_ghost):
-        ghost = load(GZ)
-        after = pltpu.roll(ghost, 127, 1)
-        before = pltpu.roll(ghost, 1, 1)
-        ahead = []
-        for q in range(nx):
-            d = load(q)
-            ahead.append(lines(d, z_up(d, ghost, q), z_dn(d, ghost, q), cz))
-            if with_ghost:
-                after = z_up_take(after, d, q)
-                before = z_dn_take(before, d, q)
-            p = q - 1
-            if p >= 0:
-                total = ahead[p][0] if p == 0 else 2.0 * ahead[p][0] + ahead[p - 1][1]
-                carry = emit(p, lap_scale * (total + ahead[q][1]), carry)
-        carry = emit(nx - 1, lap_scale * (ahead[nx - 1][0] + ahead[nx - 2][1]), carry)
-        if with_ghost:
-            inner, outer = lines(ghost, after, before, czg)
-            total = cxg * inner + jnp.where(lane >= 16, plane_dn(outer), 0.0)
-            total = total + jnp.where(lane < 16 * (nx - 1), plane_up(outer), 0.0)
-            emit(GZ, lap_scale * total, carry)
-        return carry
-
-    def reaction_of(q):
-        return TOUGHNESS / LENGTH_SCALE + 2.0 * react[q]
-
-    def old_damage(q):
-        return load_rows(3, q)
-
     def dstart(q, lap, dot):
         reaction = reaction_of(q)
         if q == GZ:
@@ -1003,7 +1011,9 @@
         return dot
 
     dvector, dgram = {}, {}
-    dvector[0] = laplace_pass(old_damage, dstart, zero, True)
+    dvector[0] = zero
+    for q in range(nx + 1):
+        dvector[0] = dstart(q, dbasis[0, q], dvector[0])
     for k in range(ng):
         more = k + 1 < ng
 

time: 20.4 us -> 20.4 us (level)
  no operation moved by 1% of the time
where the time goes in v6:
time: 20.4 us; the launch traced here: 20.2 us
  Pallas kernels  19.6 us (96%)
  between operations  0.64 us (3%)
    pallas_call x1, Pallas kernels, body_fused(): pl.pallas_call(functools.partial(kernel, sizes), out_shape=(pltpu.VMEM((3...  18.9 us
    pallas_call x1, Pallas kernels, body_fused(): pl.pallas_call(hand_on, out_shape=tuple((jax.ShapeDtypeStruct(r.shape, f3...  0.69 us

profile of v6, /device:TPU:0, one launch (start us, length us, event | category | flops | bytes accessed | tf_op | source)
XLA Modules:
  0.0 20.2 jit_solution(12606675665654022954)
XLA Ops:
  0.6 18.9 %shard_map.85 = (f32[3,4,16,128]{3,2,1,0:T(8,128)S(1)}, f32[4,16,128]{2,1,0:T(8,128)S(1)}, f32[4,16,128]{2,1,0:T(8,128)S(1)}) custom-call(f32[3,4,16,128]{3,2,1,0:T(8,128)} %disp_in.1, f32[3,4,16,128]{3,2,1,0:T(8,128)} %force_in.1, f32[4,16,128]{2,1,0:T(8,128)} %damage_in.1, f32[4,16,128]{2,1,0:T(8,128)} %history_in.1, s32[4,16,128]{2,1,0:T(8,128)} %labels_in.1, ...), custom_call_target="tpu_custom_call" | custom-call | tf_op jit(solution)/shard_map/pallas_call | solution.py:1182
  19.5 0.7 %shard_map.86 = (f32[3,4,16,128]{3,2,1,0:T(8,128)}, f32[4,16,128]{2,1,0:T(8,128)}, f32[4,16,128]{2,1,0:T(8,128)}) custom-call(f32[3,4,16,128]{3,2,1,0:T(8,128)S(1)} %get-tuple-element.6.refs_0_, f32[4,16,128]{2,1,0:T(8,128)S(1)} %get-tuple-element.7.refs_1_, f32[4,16,128]{2,1,0:T(8,128)S(1)} %get-tuple-element.8.refs_2_), custom_call_target="tpu_custom_call" | custom-call | tf_op jit(solution)/shard_map/pallas_call | solution.py:1244
